TPU v7x, 32 devices: a whole 2x2x4 slice. The times are simulated.
32 devices in a mesh: gx: 2 (over y), gy: 4 (over z), gz: 4 (over x, core).
Axes of the slice: x: 2, y: 2, z: 4, core: 2. Of those that a mesh axis runs over, the one named last changes fastest.
Arguments:
- tokens: bfloat16 [512, 6144], P(('gx', 'gy'), 'gz'), may hold values from -6 to 6
- grad_out: bfloat16 [512, 6144], P(('gx', 'gy'), 'gz'), may hold values from -1.5 to 1.5
- w_in: bfloat16 [6144, 12288], P('gz', ('gy', 'gx')), may hold values from -0.078125 to 0.078125
- w_out: bfloat16 [12288, 6144], P(('gy', 'gx'), 'gz'), may hold values from -0.0546875 to 0.0546875
Outputs:
- mlp_out: bfloat16 [512, 6144], P(('gx', 'gy'), 'gz')
- tok_grad: bfloat16 [512, 6144], P(('gx', 'gy'), 'gz')
- win_grad: float32 [6144, 12288], P('gz', ('gy', 'gx'))
- wout_grad: float32 [12288, 6144], P(('gy', 'gx'), 'gz')
All inputs are finite; a program needn't handle non-finite values.
Results may differ from a plain program's by a relative error of at most 0.01.
Values may be sent and summed in bfloat16 or wider, within the bound.
A program may use at most 128 MiB of HBM per device.

v0:
```python
import functools
import math

import jax
import jax.numpy as jnp
from jax import lax
from jax.experimental import pallas as pl
from jax.experimental.pallas import tpu as pltpu
from jax.sharding import PartitionSpec as P

MESH = pl.DeviceIdType.MESH
F32, BF16 = jnp.float32, jnp.bfloat16


def contract(left, right, dims):
    return lax.dot_general(left, right, (dims, ((), ())), preferred_element_type=F32)


def ring_kernel(
    nx, ny, nz,
    tok_ref, grad_ref, win_ref, wout_ref,
    mlp_ref, tgrad_ref, tok_out, grad_out, act_out, dpre_out,
    rows_all, win, wout, part, pair_in, paired, part_in, hid_all, send_out, own, fold_in, fold, last_in,
    local, a_z, a_x, p_sem, b_sem, c_sem, d_x, d_z,
):
    x, y, z = lax.axis_index("gx"), lax.axis_index("gy"), lax.axis_index("gz")
    t, width = tok_ref.shape
    hidden = win_ref.shape[1]
    rows = ny * t
    slab = rows // nz
    half = nz // 2
    core, chip = lax.rem(z, 2), lax.div(z, 2)
    partner = z + 1 - 2 * core
    mine_at = core * half + chip
    sends = []

    def block(e):
        return lax.rem(x - e + nx, nx)

    def peer(me, d, n):
        return lax.rem(me + d, n)

    def source(me, d, n):
        return lax.rem(me - d + n, n)

    def remote(src, dst, sems, index, device):
        return pltpu.make_async_remote_copy(
            src_ref=src, dst_ref=dst, send_sem=sems.at[(0, *index)],
            recv_sem=sems.at[(1, *index)], device_id=device, device_id_type=MESH,
        )

    def send(*args):
        copy = remote(*args)
        copy.start()
        sends.append(copy)

    stage = [
        pltpu.make_async_copy(tok_ref, rows_all.at[0, x, y], local.at[0]),
        pltpu.make_async_copy(grad_ref, rows_all.at[1, x, y], local.at[1]),
        pltpu.make_async_copy(win_ref, win, local.at[2]),
        pltpu.make_async_copy(wout_ref, wout, local.at[3]),
    ]
    for copy in stage:
        copy.start()
    barrier = pltpu.get_barrier_semaphore()
    for name, me, n in (("gx", x, nx), ("gy", y, ny), ("gz", z, nz)):
        for d in range(1, n):
            pl.semaphore_signal(
                barrier, inc=1, device_id={name: peer(me, d, n)}, device_id_type=MESH
            )
    pl.semaphore_wait(barrier, nx + ny + nz - 3)

    def across(arr, d):
        slot = rows_all.at[arr, x, source(y, d, ny)]
        for e in range(1, nx):
            send(slot, slot, a_x, (arr, e, d), {"gx": peer(x, e, nx)})

    for arr in range(2):
        stage[arr].wait()
        mine = rows_all.at[arr, x, y]
        for d in range(1, ny):
            send(mine, mine, a_z, (arr, d), {"gy": peer(y, d, ny)})
        across(arr, 0)

    def tiles(size, body, base=0):
        tile = 256 if size % 256 == 0 else 128

        def step(i, carry):
            body(pl.ds(pl.multiple_of(base + i * tile, 128), tile))
            return carry

        lax.fori_loop(0, size // tile, step, 0)

    def project(arr, e):
        left = rows_all.at[arr, block(e)]

        def body(cols):
            lhs = left[...].reshape(rows, width)
            if arr == 0:
                out = contract(lhs, win[:, cols], ((1,), (0,)))
            else:
                out = contract(lhs, wout[cols, :], ((1,), (1,)))
            part[arr, e, :, :, cols] = out.astype(BF16).reshape(nz, slab, -1)

        tiles(hidden, body)
        got = pair_in.at[arr, e]
        theirs = part.at[arr, e, pl.ds((1 - core) * half, half)]
        send(theirs, got, p_sem, (arr, e), {"gz": partner})
        remote(got, got, p_sem, (arr, e), {"gz": z}).wait_recv()

        def join(cols):
            for d in range(half):
                total = part[arr, e, core * half + d, :, cols].astype(F32)
                total = total + pair_in[arr, e, d, :, cols].astype(F32)
                paired[arr, e, d, :, cols] = total.astype(BF16)

        tiles(hidden, join)
        for d in range(1, half):
            to = peer(chip, d, half)
            send(
                paired.at[arr, e, to], part_in.at[arr, e, d], b_sem, (arr, e, d),
                {"gz": 2 * to + core},
            )

    for arr in range(2):
        for d in range(1, ny):
            slot = rows_all.at[arr, x, source(y, d, ny)]
            remote(slot, slot, a_z, (arr, d), {"gy": y}).wait_recv()
            across(arr, d)
        stage[2 + arr].wait()
        project(arr, 0)

    def activate(e):
        for arr in range(2):
            for d in range(1, half):
                got = part_in.at[arr, e, d]
                remote(got, got, b_sem, (arr, e, d), {"gz": z}).wait_recv()
        g = block(e)

        def body(cols):
            pre = paired[0, e, chip, :, cols].astype(F32)
            d_act = paired[1, e, chip, :, cols].astype(F32)
            for d in range(1, half):
                pre = pre + part_in[0, e, d, :, cols].astype(F32)
                d_act = d_act + part_in[1, e, d, :, cols].astype(F32)
            cdf = 0.5 * (1.0 + lax.erf(pre * 0.7071067811865476))
            density = jnp.exp(-0.5 * pre * pre) * 0.3989422804014327
            hid_all[0, g, mine_at, :, cols] = (pre * cdf).astype(BF16)
            hid_all[1, g, mine_at, :, cols] = (d_act * (cdf + pre * density)).astype(BF16)

        tiles(hidden, body)
        for arr in range(2):
            mine = hid_all.at[arr, g, mine_at]
            for d in range(1, half):
                to = peer(chip, d, half)
                send(mine, mine, c_sem, (arr, e, d), {"gz": 2 * to + core})
            send(mine, mine, c_sem, (arr, e, 0), {"gz": partner})

    def relay(arr, e):
        for d in range(1, half):
            slot = hid_all.at[arr, block(e), core * half + source(chip, d, half)]
            remote(slot, slot, c_sem, (arr, e, d), {"gz": z}).wait_recv()
            send(slot, slot, c_sem, (arr, e, half - 1 + d), {"gz": partner})

    for e in range(1, nx):
        for arr in range(2):
            for d in range(ny):
                slot = rows_all.at[arr, block(e), source(y, d, ny)]
                remote(slot, slot, a_x, (arr, e, d), {"gx": x}).wait_recv()
            project(arr, e)
    stores = [
        pltpu.make_async_copy(rows_all.at[0], tok_out, local.at[4]),
        pltpu.make_async_copy(rows_all.at[1], grad_out, local.at[5]),
    ]
    for copy in stores:
        copy.start()
    order = [*range(1, nx), 0]
    for e in [0, *range(1, nx)]:
        activate(e)
    for e in order:
        for arr in range(2):
            relay(arr, e)

    def expand(arr, e, keep):
        g = block(e)
        for d in range(half):
            got = hid_all.at[arr, g, (1 - core) * half + source(chip, d, half)]
            index = half - 1 + d if d else 0
            remote(got, got, c_sem, (arr, e, index), {"gz": z}).wait_recv()
        left = hid_all.at[arr, g]

        def body(cols):
            lhs = left[...].reshape(rows, hidden)
            if arr == 0:
                out = contract(lhs, wout[:, cols], ((1,), (0,)))
            else:
                out = contract(lhs, win[cols, :], ((1,), (1,)))
            if keep:
                own[arr, :, :, cols] = out.reshape(ny, t, -1)
            else:
                send_out[arr, e, :, :, cols] = out.astype(BF16).reshape(ny, t, -1)

        for q in range(2):
            view = pl.ds(q * (width // 2), width // 2)
            tiles(width // 2, body, q * (width // 2))
            if not keep:
                send(
                    send_out.at[arr, e, :, :, view], fold_in.at[arr, e, :, :, view],
                    d_x, (arr, e, q), {"gx": g},
                )

    for e in order:
        for arr in range(2):
            expand(arr, e, e == 0)
    for arr, out in enumerate((act_out, dpre_out)):
        stores.append(pltpu.make_async_copy(hid_all.at[arr], out, local.at[6 + arr]))
        stores[-1].start()
    def add(arr, cols):
        total = own[arr, :, :, cols]
        for e in range(1, nx):
            total = total + fold_in[arr, e, :, :, cols].astype(F32)
        own[arr, :, :, cols] = total
        fold[arr, :, :, cols] = total.astype(BF16)

    for arr in range(2):
        for q in range(2):
            view = pl.ds(q * (width // 2), width // 2)
            for e in range(1, nx):
                got = fold_in.at[arr, e, :, :, view]
                remote(got, got, d_x, (arr, e, q), {"gx": x}).wait_recv()
            tiles(width // 2, functools.partial(add, arr), q * (width // 2))
            for d in range(1, ny):
                to = peer(y, d, ny)
                send(
                    fold.at[arr, to, :, view], last_in.at[arr, d, :, view],
                    d_z, (arr, d, q), {"gy": to},
                )
    for arr, out in enumerate((mlp_ref, tgrad_ref)):
        for d in range(1, ny):
            for q in range(2):
                got = last_in.at[arr, d, :, pl.ds(q * (width // 2), width // 2)]
                remote(got, got, d_z, (arr, d, q), {"gy": y}).wait_recv()
        total = own[arr, y]
        for d in range(1, ny):
            total = total + last_in[arr, d].astype(F32)
        out[...] = total.astype(BF16)
    for copy in sends:
        copy.wait_send()
    for copy in stores:
        copy.wait()


def per_device(nx, ny, nz, tokens, grad_out, w_in, w_out):
    t, width = tokens.shape
    hidden = w_in.shape[1]
    rows = ny * t
    slab = rows // nz
    scale = 1.0 / math.sqrt(rows)
    anywhere = pl.BlockSpec(memory_space=pl.ANY)
    vmem = pl.BlockSpec(memory_space=pltpu.VMEM)
    dma = lambda *shape: pltpu.SemaphoreType.DMA((2, *shape))
    shape = jax.ShapeDtypeStruct
    mlp_out, tok_grad, tok_all, grad_all, act_all, d_pre_all = pl.pallas_call(
        functools.partial(ring_kernel, nx, ny, nz),
        out_shape=(
            shape((t, width), BF16), shape((t, width), BF16),
            shape((nx, ny, t, width), BF16), shape((nx, ny, t, width), BF16),
            shape((nx, nz, slab, hidden), BF16), shape((nx, nz, slab, hidden), BF16),
        ),
        in_specs=[anywhere] * 4,
        out_specs=(vmem, vmem, anywhere, anywhere, anywhere, anywhere),
        scratch_shapes=[
            pltpu.VMEM((2, nx, ny, t, width), BF16),
            pltpu.VMEM(w_in.shape, BF16),
            pltpu.VMEM(w_out.shape, BF16),
            pltpu.VMEM((2, nx, nz, slab, hidden), BF16),
            pltpu.VMEM((2, nx, nz // 2, slab, hidden), BF16),
            pltpu.VMEM((2, nx, nz // 2, slab, hidden), BF16),
            pltpu.VMEM((2, nx, nz // 2, slab, hidden), BF16),
            pltpu.VMEM((2, nx, nz, slab, hidden), BF16),
            pltpu.VMEM((2, nx, ny, t, width), BF16),
            pltpu.VMEM((2, ny, t, width), F32),
            pltpu.VMEM((2, nx, ny, t, width), BF16),
            pltpu.VMEM((2, ny, t, width), BF16),
            pltpu.VMEM((2, ny, t, width), BF16),
            pltpu.SemaphoreType.DMA((8,)),
            dma(2, ny), dma(2, nx, ny), dma(2, nx), dma(2, nx, nz), dma(2, nx, nz), dma(2, nx, 2), dma(2, ny, 2),
        ],
        compiler_params=pltpu.CompilerParams(
            collective_id=0, has_side_effects=True, vmem_limit_bytes=60 * 2**20
        ),
    )(tokens, grad_out, w_in, w_out)
    tok_all, grad_all = tok_all.reshape(-1, width), grad_all.reshape(-1, width)
    act_all, d_pre_all = act_all.reshape(-1, hidden), d_pre_all.reshape(-1, hidden)
    wout_grad = contract(act_all, grad_all, ((0,), (0,))) * scale
    win_grad = contract(tok_all, d_pre_all, ((0,), (0,))) * scale
    return mlp_out, tok_grad, win_grad, wout_grad


def solution(mesh):
    rows_spec = P(("gx", "gy"), "gz")
    in_spec = P("gz", ("gy", "gx"))
    out_spec = P(("gy", "gx"), "gz")
    sizes = (mesh.shape["gx"], mesh.shape["gy"], mesh.shape["gz"])
    return jax.shard_map(
        functools.partial(per_device, *sizes),
        mesh=mesh,
        in_specs=(rows_spec, rows_spec, in_spec, out_spec),
        out_specs=(rows_spec, rows_spec, in_spec, out_spec),
        check_vma=False,
    )
```

profile of v0, /device:TPU:0, one launch (start us, length us, event | category | flops | bytes accessed | tf_op | source)
XLA Modules:
  0.0 140.0 jit_solution(15650024409753496872)
XLA Ops:
  0.6 124.4 %shard_map.75 = (bf16[64,1536]{1,0:T(8,128)(2,1)}, bf16[64,1536]{1,0:T(8,128)(2,1)}, bf16[2,4,64,1536]{3,2,1,0:T(8,128)(2,1)}, bf16[2,4,64,1536]{3,2,1,0:T(8,128...) custom-call(bf16[64,1536]{1,0:T(8,128)(2,1)} %tok_ref.1, bf16[64,1536]{1,0:T(8,128)(2,1)} %grad_ref.1, ...), custom_call_target="tpu_custom_call" | custom-call | tf_op jit(solution)/shard_map/pallas_call | solution.py:263
  125.0 0.0 copy-start.2
  125.0 0.0 copy-start.3
  125.0 8.4 %bitcast_multiply_fusion.1 = f32[1536,1536]{1,0:T(8,128)} fusion(bf16[2,4,64,1536]{3,2,1,0:T(8,128)(2,1)} %get-tuple-element.12, bf16[2,4,64,1536]{3,2,1,0:T(8,128)(2,1)} %get-tuple-element.13), kind=kOutput, calls=%fused_computation.1 | convolution fusion | flops 2418278400 | bytes 12582912 | tf_op jit(solution)/shard_map/dot_general | solution.py:16
  133.5 0.0 copy-done.2
  133.5 0.0 copy-done.3
  133.5 0.0 copy-start.1
  133.5 0.0 copy-start
  133.5 5.2 %bitcast_multiply_fusion = f32[1536,1536]{1,0:T(8,128)} fusion(bf16[2,4,64,1536]{3,2,1,0:T(8,128)(2,1)S(1)} %copy-done.3, bf16[2,4,64,1536]{3,2,1,0:T(8,128)(2,1)S(1)} %copy-done.2), kind=kOutput, calls=%fused_computation | convolution fusion | flops 2418278400 | bytes 12582912 | tf_op jit(solution)/shard_map/dot_general | solution.py:16
  138.7 0.0 copy-done.1
  138.7 0.7 copy.12
  139.4 0.0 copy-done
  139.4 0.7 copy.13
Async XLA Ops:
  125.0 8.4 %copy-start.2 = (bf16[2,4,64,1536]{3,2,1,0:T(8,128)(2,1)S(1)}, bf16[2,4,64,1536]{3,2,1,0:T(8,128)(2,1)}, u32[]{:S(2)}) copy-start(bf16[2,4,64,1536]{3,2,1,0:T(8,128)(2,1)} %get-tuple-element.15) | copy-start | bytes 4718596
  125.0 8.4 %copy-start.3 = (bf16[2,4,64,1536]{3,2,1,0:T(8,128)(2,1)S(1)}, bf16[2,4,64,1536]{3,2,1,0:T(8,128)(2,1)}, u32[]{:S(2)}) copy-start(bf16[2,4,64,1536]{3,2,1,0:T(8,128)(2,1)} %get-tuple-element.14) | copy-start | bytes 4718596
  133.5 5.2 %copy-start.1 = (bf16[64,1536]{1,0:T(8,128)(2,1)S(1)}, bf16[64,1536]{1,0:T(8,128)(2,1)}, u32[]{:S(2)}) copy-start(bf16[64,1536]{1,0:T(8,128)(2,1)} %get-tuple-element.20) | copy-start | bytes 589828
  133.5 5.9 %copy-start = (bf16[64,1536]{1,0:T(8,128)(2,1)S(1)}, bf16[64,1536]{1,0:T(8,128)(2,1)}, u32[]{:S(2)}) copy-start(bf16[64,1536]{1,0:T(8,128)(2,1)} %get-tuple-element.21) | copy-start | bytes 589828
where the time goes:
time: 140 us
  Pallas kernels  124 us (89%)
  matrix products  13.6 us (10%)
    pallas_call x1, Pallas kernels, per_device(): pl.pallas_call(functools.partial(ring_kernel, nx, ny, nz), out_shape=(sha...  124 us
    dot_general x2, matrix products, contract(): lax.dot_general(left, right, (dims, ((), ())), preferred_element_type=F32)  13.6 us

commit v1 on v0

v1 whole, which is shorter than its diff:
```python
import functools
import math

import jax
import jax.numpy as jnp
from jax import lax
from jax.experimental import pallas as pl
from jax.experimental.pallas import tpu as pltpu
from jax.sharding import PartitionSpec as P

MESH = pl.DeviceIdType.MESH
F32, BF16 = jnp.float32, jnp.bfloat16

GATHER_VIA = (True, False)
REDUCE_VIA = (True, False)
PIECES = 2
CHUNKS = 2


def contract(left, right, dims):
    return lax.dot_general(left, right, (dims, ((), ())), preferred_element_type=F32)


def order_table(ny):
    centre = (ny - 1) / 2
    return [
        sorted(range(ny), key=lambda k: (abs(k - z), abs(k - centre))) for z in range(ny)
    ]


def schedule(ny):
    last = ny - 1
    steps = [("Fo", 0, 0), ("Fy", 1, 0), ("Fo", 0, 1), ("Fc", 0, 0), ("Fz", 1, 0), ("P", 0, 0)]
    steps += [("Fo", 0, 2), ("J", 0, 0), ("Fc", 0, 1), ("P", 0, 1), ("Fo", 1, 1), ("Fc", 1, 0)]
    steps += [("Fo", 0, 3), ("J", 0, 1), ("Fc", 0, 2), ("P", 0, 2), ("G", 0, 0), ("J", 0, 2)]
    steps += [("P", 1, 0), ("Fo", 1, 2), ("Fc", 0, 3), ("P", 0, 3), ("J", 1, 0), ("G", 0, 1), ("J", 0, 3)]
    steps += [("E", 0, 0), ("Fc", 1, 1), ("P", 1, 1), ("Fo", 1, 3), ("G", 0, 2), ("J", 1, 1)]
    steps += [("E", 0, 1), ("Fc", 1, 2), ("P", 1, 2), ("G", 0, 3), ("J", 1, 2), ("G", 1, 0)]
    steps += [("E", 0, 2), ("E", 0, 3), ("Fc", 1, 3), ("P", 1, 3), ("S", 0, 0), ("G", 1, 1), ("J", 1, 3)]
    steps += [("X", 0, 0), ("E", 1, 0), ("R", 0, 3), ("E", 1, 1), ("R", 0, 2), ("G", 1, 2), ("E", 1, 2)]
    steps += [("R", 0, 1), ("G", 1, 3), ("E", 1, 3), ("S", 1, 0), ("X", 1, 0), ("R", 0, 0)]
    steps += [("R", 1, 3), ("R", 1, 2), ("R", 1, 1), ("R", 1, 0)]
    return steps


def simple_schedule(ny):
    steps = []
    for arr in range(2):
        steps += [("Fo", arr, i) for i in range(ny)] if arr == 0 else [("Fy", 1, 0), ("Fz", 1, 0)]
        if arr == 1:
            steps += [("Fo", arr, i) for i in range(1, ny)]
        steps += [("Fc", arr, i) for i in range(ny)]
        for name in "PJGE":
            steps += [(name, arr, i) for i in range(ny)]
        steps += [("S", arr, 0), ("X", arr, 0)]
    for arr in range(2):
        steps += [("R", arr, i) for i in reversed(range(ny))]
    return steps


def ring_kernel(
    nx, ny, nz,
    tok_ref, grad_ref, win_ref, wout_ref,
    mlp_ref, tgrad_ref, tok_out, grad_out, act_out, dpre_out,
    rows_all, win, wout, part, pair_in, paired, part_in, slope, hid,
    mine_sum, cross, y_in, z_in, v_in, fold,
    local, a_y, a_z, a_v, p_sem, b_sem, c_sem, d_y, d_z, d_v,
):
    x, y, z = lax.axis_index("gx"), lax.axis_index("gy"), lax.axis_index("gz")
    t, width = tok_ref.shape
    hidden = win_ref.shape[1]
    rows = nx * t
    share = rows // 2
    half = nz // 2
    chunks = CHUNKS if hidden % (128 * CHUNKS) == 0 else 1
    core, chip = lax.rem(z, 2), lax.div(z, 2)
    partner = z + 1 - 2 * core
    sends = []

    def pick(values):
        total = 0
        for at, value in enumerate(values):
            total = total + jnp.where(y == at, value, 0)
        return total

    table = order_table(ny)
    near = [pick([table[at][i] for at in range(ny)]) for i in range(ny)]
    gap = [pick([abs(table[at][i] - at) for at in range(ny)]) for i in range(ny)]
    gaps = [{abs(table[at][i] - at) for at in range(ny)} for i in range(ny)]
    heading = [jnp.where(near[i] < y, 0, 1) for i in range(ny)]
    step_of = [1 - 2 * heading[i] for i in range(ny)]
    beyond = [
        jnp.logical_or(
            jnp.logical_and(near[i] < y, y < ny - 1), jnp.logical_and(near[i] > y, y > 0)
        )
        for i in range(ny)
    ]
    has_up, has_down = y < ny - 1, y > 0

    def via(flags, arr, i):
        if not flags[arr] or i == 0 or 1 not in gaps[i]:
            return False
        if gaps[i] == {1}:
            return True
        return gap[i] == 1

    def when(pred, body):
        if pred is True:
            body()
        elif pred is not False:
            pl.when(pred)(body)

    def negate(pred):
        return (not pred) if isinstance(pred, bool) else jnp.logical_not(pred)

    def remote(src, dst, sems, index, device):
        return pltpu.make_async_remote_copy(
            src_ref=src, dst_ref=dst, send_sem=sems.at[(0, *index)],
            recv_sem=sems.at[(1, *index)], device_id=device, device_id_type=MESH,
        )

    def send(src, dst, sems, index, device, pred=True):
        if pred is False:
            return
        copy = remote(src, dst, sems, index, device)
        when(pred, copy.start)
        sends.append((pred, copy))

    def arrive(ref, sems, index):
        remote(ref, ref, sems, index, {"gz": z}).wait_recv()

    def peer(e):
        return {"gx": lax.rem(x + e, nx)}

    def piece(p):
        return pl.ds(p * (width // PIECES), width // PIECES)

    def chunk(c):
        return pl.ds(c * (hidden // chunks), hidden // chunks)

    def tiles(size, body, base=0):
        tile = 256 if size % 256 == 0 else 128

        def step(i, carry):
            body(pl.ds(pl.multiple_of(base + i * tile, 128), tile))
            return carry

        lax.fori_loop(0, size // tile, step, 0)

    stage = [
        pltpu.make_async_copy(tok_ref, rows_all.at[0, y, 0], local.at[0]),
        pltpu.make_async_copy(grad_ref, rows_all.at[1, y, 0], local.at[1]),
        pltpu.make_async_copy(win_ref, win, local.at[2]),
        pltpu.make_async_copy(wout_ref, wout, local.at[3]),
    ]
    for copy in stage:
        copy.start()
    barrier = pltpu.get_barrier_semaphore()
    for name, me, n in (("gx", x, nx), ("gy", y, ny), ("gz", z, nz)):
        for d in range(1, n):
            pl.semaphore_signal(
                barrier, inc=1, device_id={name: lax.rem(me + d, n)}, device_id_type=MESH
            )
    pl.semaphore_wait(barrier, nx + ny + nz - 3)
    stores = []

    def to_columns(arr, i, p, pred=True):
        block = rows_all.at[arr, near[i], 0, :, piece(p)]
        for e in range(1, nx):
            dst = rows_all.at[arr, near[i], nx - e, :, piece(p)]
            send(block, dst, a_y, (arr, i, nx - e, p), peer(e), pred)

    def own_columns(arr):
        stage[arr].wait()
        for p in range(PIECES):
            to_columns(arr, 0, p)

    def own_line(arr):
        for p in range(PIECES):
            block = rows_all.at[arr, y, 0, :, piece(p)]
            send(block, block, a_z, (arr, 0, y, p), {"gy": y + 1}, has_up)
            send(block, block, a_z, (arr, 1, y, p), {"gy": y - 1}, has_down)

    def own_column(arr, i):
        if i == 0:
            own_columns(arr)
            own_line(arr)
            return
        for p in range(PIECES):
            block = rows_all.at[arr, near[i], 0, :, piece(p)]
            arrive(block, a_z, (arr, heading[i], near[i], p))
            send(
                block, block, a_z, (arr, heading[i], near[i], p),
                {"gy": y + step_of[i]}, beyond[i],
            )
            to_columns(arr, i, p, negate(via(GATHER_VIA, arr, i)))

    def other_columns(arr, i):
        by_line = via(GATHER_VIA, arr, i)
        for p in range(PIECES):
            for e in range(1, nx):
                block = rows_all.at[arr, near[i], e, :, piece(p)]
                when(by_line, lambda: arrive(block, a_v, (arr, heading[i], e, p)))
                when(negate(by_line), lambda: arrive(block, a_y, (arr, i, e, p)))
                if i == 0 and GATHER_VIA[arr]:
                    send(block, block, a_v, (arr, 0, e, p), {"gy": y + 1}, has_up)
                    send(block, block, a_v, (arr, 1, e, p), {"gy": y - 1}, has_down)

    def project(arr, i):
        if i == 0:
            stage[2 + arr].wait()
        left = rows_all.at[arr, near[i]]

        def body(cols):
            lhs = left[...].reshape(rows, width)
            if arr == 0:
                out = contract(lhs, win[:, cols], ((1,), (0,)))
            else:
                out = contract(lhs, wout[cols, :], ((1,), (1,)))
            part[arr, i, :, :, cols] = out.astype(BF16).reshape(2, share, -1)

        for c in range(chunks):
            tiles(hidden // chunks, body, c * (hidden // chunks))
            send(
                part.at[arr, i, 1 - core, :, chunk(c)], pair_in.at[arr, i, :, chunk(c)],
                p_sem, (arr, i, c), {"gz": partner},
            )

    def join(arr, i):
        def body(cols):
            total = part[arr, i, core, :, cols].astype(F32)
            total = total + pair_in[arr, i, :, cols].astype(F32)
            paired[arr, i, :, cols] = total.astype(BF16)

        for c in range(chunks):
            arrive(pair_in.at[arr, i, :, chunk(c)], p_sem, (arr, i, c))
            tiles(hidden // chunks, body, c * (hidden // chunks))
            for d in range(1, half):
                to = lax.rem(chip + d, half)
                send(
                    paired.at[arr, i, :, chunk(c)], part_in.at[arr, i, d, :, chunk(c)],
                    b_sem, (arr, i, d, c), {"gz": 2 * to + core},
                )

    def activate(arr, i):
        def body(cols):
            total = paired[arr, i, :, cols].astype(F32)
            for d in range(1, half):
                total = total + part_in[arr, i, d, :, cols].astype(F32)
            if arr == 0:
                cdf = 0.5 * (1.0 + lax.erf(total * 0.7071067811865476))
                density = jnp.exp(-0.5 * total * total) * 0.3989422804014327
                slope[i, :, cols] = cdf + total * density
                hid[arr, i, core, :, cols] = (total * cdf).astype(BF16)
            else:
                hid[arr, i, core, :, cols] = (total * slope[i, :, cols]).astype(BF16)

        for c in range(chunks):
            for d in range(1, half):
                arrive(part_in.at[arr, i, d, :, chunk(c)], b_sem, (arr, i, d, c))
            tiles(hidden // chunks, body, c * (hidden // chunks))
            mine = hid.at[arr, i, core, :, chunk(c)]
            send(mine, mine, c_sem, (arr, i, c), {"gz": partner})

    def expand(arr, i):
        for c in range(chunks):
            arrive(hid.at[arr, i, 1 - core, :, chunk(c)], c_sem, (arr, i, c))
        left = hid.at[arr, i]

        def body(cols):
            lhs = left[...].reshape(rows, hidden)
            if arr == 0:
                out = contract(lhs, wout[:, cols], ((1,), (0,)))
            else:
                out = contract(lhs, win[cols, :], ((1,), (1,)))
            mine_sum[arr, i, :, cols] = out[:t]
            for e in range(1, nx):
                cross[arr, i, e - 1, :, cols] = out[e * t:(e + 1) * t].astype(BF16)

        by_line = via(REDUCE_VIA, arr, i)
        for p in range(PIECES):
            tiles(width // PIECES, body, p * (width // PIECES))
            if i == 0 and REDUCE_VIA[arr]:
                continue
            for e in range(1, nx):
                src = cross.at[arr, i, e - 1, :, piece(p)]
                turn = 1 - heading[i]
                send(
                    src, v_in.at[arr, turn, e - 1, :, piece(p)], d_v, (arr, turn, e, p),
                    {"gy": y - step_of[i]}, by_line,
                )
                send(
                    src, y_in.at[arr, i, nx - e - 1, :, piece(p)], d_y, (arr, i, nx - e, p),
                    peer(e), negate(by_line),
                )

    def own_cross(arr):
        if not REDUCE_VIA[arr]:
            return
        for p in range(PIECES):
            for e in range(1, nx):
                for turn, pred in ((0, has_down), (1, has_up)):
                    def take(turn=turn):
                        got = v_in.at[arr, turn, e - 1, :, piece(p)]
                        arrive(got, d_v, (arr, turn, e, p))

                        def body(cols):
                            total = cross[arr, 0, e - 1, :, cols].astype(F32)
                            total = total + v_in[arr, turn, e - 1, :, cols].astype(F32)
                            cross[arr, 0, e - 1, :, cols] = total.astype(BF16)

                        tiles(width // PIECES, body, p * (width // PIECES))

                    when(pred, take)
                src = cross.at[arr, 0, e - 1, :, piece(p)]
                send(
                    src, y_in.at[arr, 0, nx - e - 1, :, piece(p)], d_y, (arr, 0, nx - e, p),
                    peer(e),
                )

    def reduce(arr, i):
        by_line = via(REDUCE_VIA, arr, i)

        def from_columns(p):
            for e in range(1, nx):
                arrive(y_in.at[arr, i, e - 1, :, piece(p)], d_y, (arr, i, e, p))

            def body(cols):
                total = mine_sum[arr, i, :, cols]
                for e in range(1, nx):
                    total = total + y_in[arr, i, e - 1, :, cols].astype(F32)
                mine_sum[arr, i, :, cols] = total

            tiles(width // PIECES, body, p * (width // PIECES))

        def from_line(p, turn, at):
            arrive(z_in.at[arr, turn, at, :, piece(p)], d_z, (arr, turn, at, p))

            def body(cols):
                total = mine_sum[arr, i, :, cols] + z_in[arr, turn, at, :, cols].astype(F32)
                mine_sum[arr, i, :, cols] = total

            tiles(width // PIECES, body, p * (width // PIECES))

        out = (mlp_ref, tgrad_ref)[arr]
        for p in range(PIECES):
            when(negate(by_line), lambda: from_columns(p))
            if i == 0:
                when(has_down, lambda: from_line(p, 0, y))
                when(has_up, lambda: from_line(p, 1, y))
                out[:, piece(p)] = mine_sum[arr, 0, :, piece(p)].astype(BF16)
                continue
            turn = 1 - heading[i]
            when(beyond[i], lambda: from_line(p, turn, near[i]))

            def body(cols):
                fold[arr, i, :, cols] = mine_sum[arr, i, :, cols].astype(BF16)

            tiles(width // PIECES, body, p * (width // PIECES))
            send(
                fold.at[arr, i, :, piece(p)], z_in.at[arr, turn, near[i], :, piece(p)],
                d_z, (arr, turn, near[i], p), {"gy": y - step_of[i]},
            )

    def store(arr):
        for src, dst, at in (
            (rows_all.at[arr], (tok_out, grad_out)[arr], 4 + arr),
        ):
            stores.append(pltpu.make_async_copy(src, dst, local.at[at]))
            stores[-1].start()
        for i in range(ny):
            out = (act_out, dpre_out)[arr].at[near[i]]
            stores.append(pltpu.make_async_copy(hid.at[arr, i], out, local.at[6 + arr * ny + i]))
            stores[-1].start()

    acts = {
        "Fo": own_column, "Fc": other_columns, "P": project, "J": join, "G": activate,
        "E": expand, "R": reduce,
        "Fy": lambda arr, i: own_columns(arr), "Fz": lambda arr, i: own_line(arr),
        "X": lambda arr, i: own_cross(arr), "S": lambda arr, i: store(arr),
    }
    for name, arr, i in (schedule(ny) if ny == 4 else simple_schedule(ny)):
        acts[name](arr, i)
    for pred, copy in sends:
        when(pred, copy.wait_send)
    for copy in stores:
        copy.wait()


def grad_kernel(scale, tok_ref, dpre_ref, act_ref, grad_ref, win_ref, wout_ref):
    win_ref[...] = contract(tok_ref[...], dpre_ref[...], ((0,), (0,))) * scale
    wout_ref[...] = contract(act_ref[...], grad_ref[...], ((0,), (0,))) * scale


def weight_grads(tok, dpre, act, grad, scale):
    tokens, width = tok.shape
    hidden = dpre.shape[1]
    steps = next(n for n in (6, 3, 2, 1) if width % (128 * n) == 0 and hidden % (128 * n) == 0)
    wide, tall = width // steps, hidden // steps
    return pl.pallas_call(
        functools.partial(grad_kernel, scale),
        grid=(steps,),
        out_shape=(
            jax.ShapeDtypeStruct((width, hidden), F32), jax.ShapeDtypeStruct((hidden, width), F32),
        ),
        in_specs=[
            pl.BlockSpec((tokens, wide), lambda i: (0, i)),
            pl.BlockSpec((tokens, hidden), lambda i: (0, 0)),
            pl.BlockSpec((tokens, tall), lambda i: (0, i)),
            pl.BlockSpec((tokens, width), lambda i: (0, 0)),
        ],
        out_specs=(
            pl.BlockSpec((wide, hidden), lambda i: (i, 0)),
            pl.BlockSpec((tall, width), lambda i: (i, 0)),
        ),
        compiler_params=pltpu.CompilerParams(vmem_limit_bytes=48 * 2**20),
        cost_estimate=pl.CostEstimate(
            flops=4 * tokens * width * hidden, transcendentals=0,
            bytes_accessed=8 * width * hidden + 4 * tokens * (width + hidden),
        ),
    )(tok, dpre, act, grad)


def per_device(nx, ny, nz, tokens, grad_out, w_in, w_out):
    t, width = tokens.shape
    hidden = w_in.shape[1]
    rows = nx * t
    share = rows // 2
    half = nz // 2
    scale = 1.0 / math.sqrt(ny * t)
    anywhere = pl.BlockSpec(memory_space=pl.ANY)
    vmem = pl.BlockSpec(memory_space=pltpu.VMEM)
    dma = lambda *shape: pltpu.SemaphoreType.DMA((2, *shape))
    shape = jax.ShapeDtypeStruct
    mlp_out, tok_grad, tok_all, grad_all, act_all, d_pre_all = pl.pallas_call(
        functools.partial(ring_kernel, nx, ny, nz),
        out_shape=(
            shape((t, width), BF16), shape((t, width), BF16),
            shape((ny, nx, t, width), BF16), shape((ny, nx, t, width), BF16),
            shape((ny, 2, share, hidden), BF16), shape((ny, 2, share, hidden), BF16),
        ),
        in_specs=[anywhere] * 4,
        out_specs=(vmem, vmem, anywhere, anywhere, anywhere, anywhere),
        scratch_shapes=[
            pltpu.VMEM((2, ny, nx, t, width), BF16),
            pltpu.VMEM(w_in.shape, BF16),
            pltpu.VMEM(w_out.shape, BF16),
            pltpu.VMEM((2, ny, 2, share, hidden), BF16),
            pltpu.VMEM((2, ny, share, hidden), BF16),
            pltpu.VMEM((2, ny, share, hidden), BF16),
            pltpu.VMEM((2, ny, half, share, hidden), BF16),
            pltpu.VMEM((ny, share, hidden), F32),
            pltpu.VMEM((2, ny, 2, share, hidden), BF16),
            pltpu.VMEM((2, ny, t, width), F32),
            pltpu.VMEM((2, ny, nx - 1, t, width), BF16),
            pltpu.VMEM((2, ny, nx - 1, t, width), BF16),
            pltpu.VMEM((2, 2, ny, t, width), BF16),
            pltpu.VMEM((2, 2, nx - 1, t, width), BF16),
            pltpu.VMEM((2, ny, t, width), BF16),
            pltpu.SemaphoreType.DMA((6 + 2 * ny,)),
            dma(2, ny, nx, PIECES), dma(2, 2, ny, PIECES), dma(2, 2, nx, PIECES),
            dma(2, ny, CHUNKS), dma(2, ny, half, CHUNKS), dma(2, ny, CHUNKS),
            dma(2, ny, nx, PIECES), dma(2, 2, ny, PIECES), dma(2, 2, nx, PIECES),
        ],
        compiler_params=pltpu.CompilerParams(
            collective_id=0, has_side_effects=True, vmem_limit_bytes=60 * 2**20
        ),
    )(tokens, grad_out, w_in, w_out)
    tok_all, grad_all = tok_all.reshape(-1, width), grad_all.reshape(-1, width)
    act_all, d_pre_all = act_all.reshape(-1, hidden), d_pre_all.reshape(-1, hidden)
    win_grad, wout_grad = weight_grads(tok_all, d_pre_all, act_all, grad_all, scale)
    return mlp_out, tok_grad, win_grad, wout_grad


def solution(mesh):
    rows_spec = P(("gx", "gy"), "gz")
    in_spec = P("gz", ("gy", "gx"))
    out_spec = P(("gy", "gx"), "gz")
    sizes = (mesh.shape["gx"], mesh.shape["gy"], mesh.shape["gz"])
    return jax.shard_map(
        functools.partial(per_device, *sizes),
        mesh=mesh,
        in_specs=(rows_spec, rows_spec, in_spec, out_spec),
        out_specs=(rows_spec, rows_spec, in_spec, out_spec),
        check_vma=False,
    )
```

time: 140 us -> 117 us (0.84)
  matrix products: 13.6 us -> 0 us
  Pallas kernels: 124 us -> 111 us
  local copies, waits for them, and re-layouts: 1.37 us -> 5.58 us
    pallas_call x1, Pallas kernels: 124 us -> 101 us  [per_device(): pl.pallas_call(functools.partial(ring_kernel, nx, ny, nz), out_shape=(sha...]
    dot_general x2 -> x0, matrix products: 13.6 us -> none  [contract(): lax.dot_general(left, right, (dims, ((), ())), preferred_element_type=F32)]
    pallas_call x0 -> x1, Pallas kernels: none -> 9.31 us  [weight_grads(): pl.pallas_call(functools.partial(grad_kernel, scale), grid=(steps,), out_...]
    unnamed x10 -> x12, local copies, waits for them, and re-layouts: 1.37 us -> 5.58 us
where the time goes in v1:
time: 117 us
  Pallas kernels  111 us (95%)
  local copies, waits for them, and re-layouts  5.58 us (5%)
    pallas_call x1, Pallas kernels, per_device(): pl.pallas_call(functools.partial(ring_kernel, nx, ny, nz), out_shape=(sha...  101 us
    pallas_call x1, Pallas kernels, weight_grads(): pl.pallas_call(functools.partial(grad_kernel, scale), grid=(steps,), out_...  9.31 us
    unnamed x12, local copies, waits for them, and re-layouts  5.58 us

profile of v1, /device:TPU:0, one launch (start us, length us, event | category | flops | bytes accessed | tf_op | source)
XLA Modules:
  0.0 116.9 jit_solution(14032479334277718358)
XLA Ops:
  0.6 101.4 %shard_map.75 = (bf16[64,1536]{1,0:T(8,128)(2,1)}, bf16[64,1536]{1,0:T(8,128)(2,1)}, bf16[4,2,64,1536]{3,2,1,0:T(8,128)(2,1)}, bf16[4,2,64,1536]{3,2,1,0:T(8,128...) custom-call(bf16[64,1536]{1,0:T(8,128)(2,1)} %tok_ref.1, bf16[64,1536]{1,0:T(8,128)(2,1)} %grad_ref.1, ...), custom_call_target="tpu_custom_call" | custom-call | tf_op jit(solution)/shard_map/pallas_call | solution.py:435
  102.0 0.0 copy-start
  102.0 1.4 %copy-done = bf16[4,2,64,1536]{3,2,1,0:T(8,128)(2,1)S(1)} copy-done((bf16[4,2,64,1536]{3,2,1,0:T(8,128)(2,1)S(1)}, bf16[4,2,64,1536]{3,2,1,0:T(8,128)(2,1)}, u32[]{:S(2)}) %copy-start) | copy-done | bytes 1572888
  103.4 0.0 copy-start.1
  103.4 1.4 %copy-done.1 = bf16[4,2,64,1536]{3,2,1,0:T(8,128)(2,1)S(1)} copy-done((bf16[4,2,64,1536]{3,2,1,0:T(8,128)(2,1)S(1)}, bf16[4,2,64,1536]{3,2,1,0:T(8,128)(2,1)}, u32[]{:S(2)}) %copy-start.1) | copy-done | bytes 1572888
  104.8 0.0 copy-start.2
  104.8 1.4 %copy-done.2 = bf16[4,2,64,1536]{3,2,1,0:T(8,128)(2,1)S(1)} copy-done((bf16[4,2,64,1536]{3,2,1,0:T(8,128)(2,1)S(1)}, bf16[4,2,64,1536]{3,2,1,0:T(8,128)(2,1)}, u32[]{:S(2)}) %copy-start.2) | copy-done | bytes 1572888
  106.2 0.0 copy-start.4
  106.2 0.0 copy-start.3
  106.2 9.3 %shard_map.76 = (f32[1536,1536]{1,0:T(8,128)}, f32[1536,1536]{1,0:T(8,128)}) custom-call(bf16[512,1536]{1,0:T(8,128)(2,1)S(1)} %bitcast.4, bf16[512,1536]{1,0:T(8,128)(2,1)S(1)} %bitcast.6, bf16[512,1536]{1,0:T(8,128)(2,1)S(1)} %bitcast.5, bf16[512,1536]{1,0:T(8,128)(2,1)} %bitcast.7), custom_call_target="tpu_custom_call" | custom-call | flops 4831838208 | bytes 25165824 | tf_op jit(solution)/shard_map/pallas_call | solution.py:400
  115.5 0.0 copy-done.4
  115.5 0.7 copy.10
  116.2 0.0 copy-done.3
  116.2 0.7 copy.11
Async XLA Ops:
  102.0 1.4 %copy-start = (bf16[4,2,64,1536]{3,2,1,0:T(8,128)(2,1)S(1)}, bf16[4,2,64,1536]{3,2,1,0:T(8,128)(2,1)}, u32[]{:S(2)}) copy-start(bf16[4,2,64,1536]{3,2,1,0:T(8,128)(2,1)} %get-tuple-element.14) | copy-start | bytes 4718596
  103.4 1.4 %copy-start.1 = (bf16[4,2,64,1536]{3,2,1,0:T(8,128)(2,1)S(1)}, bf16[4,2,64,1536]{3,2,1,0:T(8,128)(2,1)}, u32[]{:S(2)}) copy-start(bf16[4,2,64,1536]{3,2,1,0:T(8,128)(2,1)} %get-tuple-element.16) | copy-start | bytes 4718596
  104.8 1.4 %copy-start.2 = (bf16[4,2,64,1536]{3,2,1,0:T(8,128)(2,1)S(1)}, bf16[4,2,64,1536]{3,2,1,0:T(8,128)(2,1)}, u32[]{:S(2)}) copy-start(bf16[4,2,64,1536]{3,2,1,0:T(8,128)(2,1)} %get-tuple-element.15) | copy-start | bytes 4718596
  106.2 9.3 %copy-start.4 = (bf16[64,1536]{1,0:T(8,128)(2,1)S(1)}, bf16[64,1536]{1,0:T(8,128)(2,1)}, u32[]{:S(2)}) copy-start(bf16[64,1536]{1,0:T(8,128)(2,1)} %get-tuple-element.24) | copy-start | bytes 589828
  106.2 10.0 %copy-start.3 = (bf16[64,1536]{1,0:T(8,128)(2,1)S(1)}, bf16[64,1536]{1,0:T(8,128)(2,1)}, u32[]{:S(2)}) copy-start(bf16[64,1536]{1,0:T(8,128)(2,1)} %get-tuple-element.25) | copy-start | bytes 589828

commit v2 on v1

v2 whole, which is shorter than its diff:
```python
import functools
import math

import jax
import jax.numpy as jnp
from jax import lax
from jax.experimental import pallas as pl
from jax.experimental.pallas import tpu as pltpu
from jax.sharding import PartitionSpec as P

MESH = pl.DeviceIdType.MESH
F32, BF16 = jnp.float32, jnp.bfloat16

GATHER_VIA = (False, False)
REDUCE_VIA = (True, False)
PIECES = 2
CHUNKS = 2
WIDE = 768
FLUSHES = 2
PLAN = (
    "Y000", "Z000", "Y001", "Z001", "W100", "Y100", "F010", "W000", "Z100", "T100", "C000",
    "C001", "F020", "F011", "P000", "P001", "F021", "T101", "F030", "C020", "J000", "F031",
    "F110", "Z101", "J001", "C010", "C100", "C011", "P010", "T000", "J010", "C021", "F120",
    "P020", "G000", "P011", "C030", "F111", "J020", "P021", "J011", "F121", "C031", "P030",
    "G010", "P031", "J030", "F130", "C110", "J031", "G001", "J021", "G020", "F131", "C111",
    "G011", "Y101", "P110", "C120", "C121", "P120", "P121", "G030", "E010", "G031", "J110",
    "E011", "P111", "C130", "E030", "C131", "G021", "P130", "P131", "E031", "C101", "J130",
    "E020", "E000", "J131", "J120", "E021", "G110", "R030", "T001", "R031", "X000", "G130",
    "G131", "J121", "P100", "E130", "R020", "J111", "P101", "G120", "E131", "R010", "R021",
    "J100", "G121", "E120", "G111", "E121", "E110", "R130", "J101", "E111", "R000", "G100",
    "R131", "E001", "R120", "X001", "G101", "R110", "E100", "R121", "R011", "E101", "R111",
    "R001", "R100", "R101",
)


def contract(left, right, dims):
    return lax.dot_general(left, right, (dims, ((), ())), preferred_element_type=F32)


def order_table(ny):
    centre = (ny - 1) / 2
    return [
        sorted(range(ny), key=lambda k: (abs(k - z), abs(k - centre))) for z in range(ny)
    ]


def schedule(ny):
    steps = [("W", 0, 0), ("W", 1, 0), ("T", 0, 0), ("T", 1, 0)]
    for arr in range(2):
        steps += [("Y", arr, 0), ("Z", arr, 0)]
        steps += [("F", arr, i) for i in range(1, ny)] + [("C", arr, i) for i in range(ny)]
        for name in "PJGE":
            steps += [(name, arr, i) for i in range(ny)]
        steps += [("X", arr, 0)]
    for arr in range(2):
        steps += [("R", arr, i) for i in reversed(range(ny))]
    steps = [(*step, p) for step in steps for p in range(PIECES) if step[0] != "W" or p == 0]
    if ny == 4:
        steps = [(step[0], *map(int, step[1:])) for step in PLAN]
    for arr in range(2):
        last = max(at for at, step in enumerate(steps) if step[:2] == ("E", arr))
        steps.insert(last + 1, ("S", arr, 0, 0))
    return steps


def ring_kernel(
    nx, ny, nz,
    tok_ref, grad_ref, win_ref, wout_ref,
    mlp_ref, tgrad_ref, tok_out, grad_out, act_out, dpre_out,
    rows_all, win, wout, win_t, wout_t, part, pair_in, paired, part_in, slope, hid,
    mine_sum, cross, y_in, z_in, v_in, fold,
    local, a_y, a_z, a_v, p_sem, b_sem, c_sem, d_y, d_z, d_v,
):
    x, y, z = lax.axis_index("gx"), lax.axis_index("gy"), lax.axis_index("gz")
    t, width = tok_ref.shape
    hidden = win_ref.shape[1]
    rows = nx * t
    share = rows // 2
    half = nz // 2
    chunks = CHUNKS if hidden % (128 * CHUNKS) == 0 else 1
    core, chip = lax.rem(z, 2), lax.div(z, 2)
    partner = z + 1 - 2 * core
    sends = []

    def pick(values):
        total = 0
        for at, value in enumerate(values):
            total = total + jnp.where(y == at, value, 0)
        return total

    table = order_table(ny)
    near = [pick([table[at][i] for at in range(ny)]) for i in range(ny)]
    gap = [pick([abs(table[at][i] - at) for at in range(ny)]) for i in range(ny)]
    gaps = [{abs(table[at][i] - at) for at in range(ny)} for i in range(ny)]
    heading = [jnp.where(near[i] < y, 0, 1) for i in range(ny)]
    step_of = [1 - 2 * heading[i] for i in range(ny)]
    beyond = [
        jnp.logical_or(
            jnp.logical_and(near[i] < y, y < ny - 1), jnp.logical_and(near[i] > y, y > 0)
        )
        for i in range(ny)
    ]
    has_up, has_down = y < ny - 1, y > 0

    def via(flags, arr, i):
        if not flags[arr] or i == 0 or 1 not in gaps[i]:
            return False
        if gaps[i] == {1}:
            return True
        return gap[i] == 1

    def when(pred, body):
        if pred is True:
            body()
        elif pred is not False:
            pl.when(pred)(body)

    def negate(pred):
        return (not pred) if isinstance(pred, bool) else jnp.logical_not(pred)

    def remote(src, dst, sems, index, device):
        return pltpu.make_async_remote_copy(
            src_ref=src, dst_ref=dst, send_sem=sems.at[(0, *index)],
            recv_sem=sems.at[(1, *index)], device_id=device, device_id_type=MESH,
        )

    def send(src, dst, sems, index, device, pred=True):
        if pred is False:
            return
        copy = remote(src, dst, sems, index, device)
        when(pred, copy.start)
        sends.append((pred, copy))

    def arrive(ref, sems, index):
        remote(ref, ref, sems, index, {"gz": z}).wait_recv()

    def peer(e):
        return {"gx": lax.rem(x + e, nx)}

    def piece(p):
        return pl.ds(p * (width // PIECES), width // PIECES)

    def chunk(c):
        return pl.ds(c * (hidden // chunks), hidden // chunks)

    def tiles(size, body, base=0, widest=256):
        tile = next(n for n in (widest, 256, 128) if size % n == 0)

        def step(i, carry):
            body(pl.ds(pl.multiple_of(base + i * tile, 128), tile))
            return carry

        lax.fori_loop(0, size // tile, step, 0)

    stage = [
        pltpu.make_async_copy(tok_ref, rows_all.at[0, y, 0], local.at[0]),
        pltpu.make_async_copy(grad_ref, rows_all.at[1, y, 0], local.at[1]),
        pltpu.make_async_copy(win_ref, win, local.at[2]),
        pltpu.make_async_copy(wout_ref, wout, local.at[3]),
    ]
    for copy in stage:
        copy.start()
    barrier = pltpu.get_barrier_semaphore()
    for name, me, n in (("gx", x, nx), ("gy", y, ny), ("gz", z, nz)):
        for d in range(1, n):
            pl.semaphore_signal(
                barrier, inc=1, device_id={name: lax.rem(me + d, n)}, device_id_type=MESH
            )
    pl.semaphore_wait(barrier, nx + ny + nz - 3)
    stores = []

    def to_columns(arr, i, p, pred=True):
        block = rows_all.at[arr, near[i], 0, :, piece(p)]
        for e in range(1, nx):
            dst = rows_all.at[arr, near[i], nx - e, :, piece(p)]
            send(block, dst, a_y, (arr, i, nx - e - 1, p), peer(e), pred)

    def own_columns(arr, i, p):
        if p == 0:
            stage[arr].wait()
        to_columns(arr, 0, p)

    def own_line(arr, i, p):
        block = rows_all.at[arr, y, 0, :, piece(p)]
        send(block, block, a_z, (arr, 0, y, p), {"gy": y + 1}, has_up)
        send(block, block, a_z, (arr, 1, y, p), {"gy": y - 1}, has_down)

    def own_column(arr, i, p):
        block = rows_all.at[arr, near[i], 0, :, piece(p)]
        arrive(block, a_z, (arr, heading[i], near[i], p))
        send(
            block, block, a_z, (arr, heading[i], near[i], p),
            {"gy": y + step_of[i]}, beyond[i],
        )
        to_columns(arr, i, p, negate(via(GATHER_VIA, arr, i)))

    def other_columns(arr, i, p):
        by_line = via(GATHER_VIA, arr, i)
        for e in range(1, nx):
            block = rows_all.at[arr, near[i], e, :, piece(p)]
            when(by_line, lambda: arrive(block, a_v, (arr, heading[i], e - 1, p)))
            when(negate(by_line), lambda: arrive(block, a_y, (arr, i, e - 1, p)))
            if i == 0 and GATHER_VIA[arr]:
                send(block, block, a_v, (arr, 0, e - 1, p), {"gy": y + 1}, has_up)
                send(block, block, a_v, (arr, 1, e - 1, p), {"gy": y - 1}, has_down)

    def turn_over(arr, i, p):
        src, dst = ((win, win_t), (wout, wout_t))[arr]
        side = src.shape[0] // PIECES
        tall = 256 if side % 256 == 0 else 128
        for j in range(side // tall):
            at = p * side + j * tall
            def body(cols):
                dst[cols, at:at + tall] = src[at:at + tall, cols].T
            tiles(src.shape[1], body)

    def project(arr, i, c):
        left = rows_all.at[arr, near[i]]

        def body(cols):
            lhs = left[...].reshape(rows, width)
            out = contract(lhs, (win, wout_t)[arr][:, cols], ((1,), (0,)))
            part[arr, i, :, :, cols] = out.astype(BF16).reshape(2, share, -1)

        tiles(hidden // chunks, body, c * (hidden // chunks), WIDE)
        send(
            part.at[arr, i, 1 - core, :, chunk(c)], pair_in.at[arr, i, :, chunk(c)],
            p_sem, (arr, i, c), {"gz": partner},
        )

    def join(arr, i, c):
        def body(cols):
            total = part[arr, i, core, :, cols].astype(F32)
            total = total + pair_in[arr, i, :, cols].astype(F32)
            paired[arr, i, :, cols] = total.astype(BF16)

        arrive(pair_in.at[arr, i, :, chunk(c)], p_sem, (arr, i, c))
        tiles(hidden // chunks, body, c * (hidden // chunks))
        for d in range(1, half):
            to = lax.rem(chip + d, half)
            send(
                paired.at[arr, i, :, chunk(c)], part_in.at[arr, i, d - 1, :, chunk(c)],
                b_sem, (arr, i, d - 1, c), {"gz": 2 * to + core},
            )

    def activate(arr, i, c):
        def body(cols):
            total = paired[arr, i, :, cols].astype(F32)
            for d in range(1, half):
                total = total + part_in[arr, i, d - 1, :, cols].astype(F32)
            if arr == 0:
                cdf = 0.5 * (1.0 + lax.erf(total * 0.7071067811865476))
                density = jnp.exp(-0.5 * total * total) * 0.3989422804014327
                slope[i, :, cols] = cdf + total * density
                hid[arr, i, core, :, cols] = (total * cdf).astype(BF16)
            else:
                hid[arr, i, core, :, cols] = (total * slope[i, :, cols]).astype(BF16)

        for d in range(1, half):
            arrive(part_in.at[arr, i, d - 1, :, chunk(c)], b_sem, (arr, i, d - 1, c))
        tiles(hidden // chunks, body, c * (hidden // chunks))
        mine = hid.at[arr, i, core, :, chunk(c)]
        send(mine, mine, c_sem, (arr, i, c), {"gz": partner})

    def expand(arr, i, p):
        if p == 0:
            for c in range(chunks):
                arrive(hid.at[arr, i, 1 - core, :, chunk(c)], c_sem, (arr, i, c))
        left = hid.at[arr, i]

        def body(cols):
            lhs = left[...].reshape(rows, hidden)
            out = contract(lhs, (wout, win_t)[arr][:, cols], ((1,), (0,)))
            mine_sum[arr, i, :, cols] = out[:t]
            for e in range(1, nx):
                cross[arr, i, e - 1, :, cols] = out[e * t:(e + 1) * t].astype(BF16)

        by_line = via(REDUCE_VIA, arr, i)
        tiles(width // PIECES, body, p * (width // PIECES), WIDE)
        if i == 0 and REDUCE_VIA[arr]:
            return
        for e in range(1, nx):
            src = cross.at[arr, i, e - 1, :, piece(p)]
            turn = 1 - heading[i]
            send(
                src, v_in.at[arr, turn, e - 1, :, piece(p)], d_v, (arr, turn, e - 1, p),
                {"gy": y - step_of[i]}, by_line,
            )
            send(
                src, y_in.at[arr, i, nx - e - 1, :, piece(p)], d_y, (arr, i, nx - e - 1, p),
                peer(e), negate(by_line),
            )

    def own_cross(arr, i, p):
        if not REDUCE_VIA[arr]:
            return
        for e in range(1, nx):
            for turn, pred in ((0, has_down), (1, has_up)):
                def take(turn=turn):
                    got = v_in.at[arr, turn, e - 1, :, piece(p)]
                    arrive(got, d_v, (arr, turn, e - 1, p))

                    def body(cols):
                        total = cross[arr, 0, e - 1, :, cols].astype(F32)
                        total = total + v_in[arr, turn, e - 1, :, cols].astype(F32)
                        cross[arr, 0, e - 1, :, cols] = total.astype(BF16)

                    tiles(width // PIECES, body, p * (width // PIECES))

                when(pred, take)
            src = cross.at[arr, 0, e - 1, :, piece(p)]
            send(
                src, y_in.at[arr, 0, nx - e - 1, :, piece(p)], d_y, (arr, 0, nx - e - 1, p),
                peer(e),
            )

    def reduce(arr, i, p):
        by_line = via(REDUCE_VIA, arr, i)

        def from_columns():
            for e in range(1, nx):
                arrive(y_in.at[arr, i, e - 1, :, piece(p)], d_y, (arr, i, e - 1, p))

            def body(cols):
                total = mine_sum[arr, i, :, cols]
                for e in range(1, nx):
                    total = total + y_in[arr, i, e - 1, :, cols].astype(F32)
                mine_sum[arr, i, :, cols] = total

            tiles(width // PIECES, body, p * (width // PIECES))

        def from_line(turn, at):
            arrive(z_in.at[arr, turn, at, :, piece(p)], d_z, (arr, turn, at, p))

            def body(cols):
                total = mine_sum[arr, i, :, cols] + z_in[arr, turn, at, :, cols].astype(F32)
                mine_sum[arr, i, :, cols] = total

            tiles(width // PIECES, body, p * (width // PIECES))

        out = (mlp_ref, tgrad_ref)[arr]
        when(negate(by_line), from_columns)
        if i == 0:
            when(has_down, lambda: from_line(0, y))
            when(has_up, lambda: from_line(1, y))
            out[:, piece(p)] = mine_sum[arr, 0, :, piece(p)].astype(BF16)
            return
        turn = 1 - heading[i]
        when(beyond[i], lambda: from_line(turn, near[i]))

        def body(cols):
            fold[arr, i, :, cols] = mine_sum[arr, i, :, cols].astype(BF16)

        tiles(width // PIECES, body, p * (width // PIECES))
        send(
            fold.at[arr, i, :, piece(p)], z_in.at[arr, turn, near[i], :, piece(p)],
            d_z, (arr, turn, near[i], p), {"gy": y - step_of[i]},
        )

    def store(arr, i, p):
        stores.append(
            pltpu.make_async_copy(rows_all.at[arr], (tok_out, grad_out)[arr], local.at[4 + arr])
        )
        stores[-1].start()
        for i in range(ny):
            out = (act_out, dpre_out)[arr].at[near[i]]
            stores.append(pltpu.make_async_copy(hid.at[arr, i], out, local.at[6 + arr * ny + i]))
            stores[-1].start()

    acts = {
        "Y": own_columns, "Z": own_line, "F": own_column, "C": other_columns, "T": turn_over,
        "P": project, "J": join, "G": activate, "E": expand, "X": own_cross, "R": reduce,
        "S": store, "W": lambda arr, i, p: stage[2 + arr].wait(),
    }
    def flush(count):
        for pred, copy in sends[:count]:
            when(pred, copy.wait_send)
        del sends[:count]

    steps = schedule(ny)
    marks = [at for at, step in enumerate(steps) if step[0] == "R"][-FLUSHES:]
    before = 0
    for at, (name, arr, i, p) in enumerate(steps):
        if name in "PJG" and p >= chunks:
            continue
        if at in marks:
            flush(before)
        before = len(sends)
        acts[name](arr, i, p)
    flush(len(sends))
    for copy in stores:
        copy.wait()


def grad_kernel(scale, tok_ref, dpre_ref, act_ref, grad_ref, win_ref, wout_ref):
    win_ref[...] = contract(tok_ref[...], dpre_ref[...], ((0,), (0,))) * scale
    wout_ref[...] = contract(act_ref[...], grad_ref[...], ((0,), (0,))) * scale


def weight_grads(tok, dpre, act, grad, scale):
    tokens, width = tok.shape
    hidden = dpre.shape[1]
    steps = next(n for n in (6, 3, 2, 1) if width % (128 * n) == 0 and hidden % (128 * n) == 0)
    wide, tall = width // steps, hidden // steps
    return pl.pallas_call(
        functools.partial(grad_kernel, scale),
        grid=(steps,),
        out_shape=(
            jax.ShapeDtypeStruct((width, hidden), F32), jax.ShapeDtypeStruct((hidden, width), F32),
        ),
        in_specs=[
            pl.BlockSpec((tokens, wide), lambda i: (0, i)),
            pl.BlockSpec((tokens, hidden), lambda i: (0, 0)),
            pl.BlockSpec((tokens, tall), lambda i: (0, i)),
            pl.BlockSpec((tokens, width), lambda i: (0, 0)),
        ],
        out_specs=(
            pl.BlockSpec((wide, hidden), lambda i: (i, 0)),
            pl.BlockSpec((tall, width), lambda i: (i, 0)),
        ),
        compiler_params=pltpu.CompilerParams(vmem_limit_bytes=60 * 2**20),
        cost_estimate=pl.CostEstimate(
            flops=4 * tokens * width * hidden, transcendentals=0,
            bytes_accessed=8 * width * hidden + 4 * tokens * (width + hidden),
        ),
    )(tok, dpre, act, grad)


def per_device(nx, ny, nz, tokens, grad_out, w_in, w_out):
    t, width = tokens.shape
    hidden = w_in.shape[1]
    rows = nx * t
    share = rows // 2
    half = nz // 2
    scale = 1.0 / math.sqrt(ny * t)
    anywhere = pl.BlockSpec(memory_space=pl.ANY)
    vmem = pl.BlockSpec(memory_space=pltpu.VMEM)
    dma = lambda *shape: pltpu.SemaphoreType.DMA((2, *shape))
    shape = jax.ShapeDtypeStruct
    mlp_out, tok_grad, tok_all, grad_all, act_all, d_pre_all = pl.pallas_call(
        functools.partial(ring_kernel, nx, ny, nz),
        out_shape=(
            shape((t, width), BF16), shape((t, width), BF16),
            shape((ny, nx, t, width), BF16), shape((ny, nx, t, width), BF16),
            shape((ny, 2, share, hidden), BF16), shape((ny, 2, share, hidden), BF16),
        ),
        in_specs=[anywhere] * 4,
        out_specs=(vmem, vmem, anywhere, anywhere, anywhere, anywhere),
        scratch_shapes=[
            pltpu.VMEM((2, ny, nx, t, width), BF16),
            pltpu.VMEM(w_in.shape, BF16),
            pltpu.VMEM(w_out.shape, BF16),
            pltpu.VMEM(w_in.shape[::-1], BF16),
            pltpu.VMEM(w_out.shape[::-1], BF16),
            pltpu.VMEM((2, ny, 2, share, hidden), BF16),
            pltpu.VMEM((2, ny, share, hidden), BF16),
            pltpu.VMEM((2, ny, share, hidden), BF16),
            pltpu.VMEM((2, ny, half - 1, share, hidden), BF16),
            pltpu.VMEM((ny, share, hidden), F32),
            pltpu.VMEM((2, ny, 2, share, hidden), BF16),
            pltpu.VMEM((2, ny, t, width), F32),
            pltpu.VMEM((2, ny, nx - 1, t, width), BF16),
            pltpu.VMEM((2, ny, nx - 1, t, width), BF16),
            pltpu.VMEM((2, 2, ny, t, width), BF16),
            pltpu.VMEM((2, 2, nx - 1, t, width), BF16),
            pltpu.VMEM((2, ny, t, width), BF16),
            pltpu.SemaphoreType.DMA((6 + 2 * ny,)),
            dma(2, ny, nx - 1, PIECES), dma(2, 2, ny, PIECES), dma(2, 2, nx - 1, PIECES),
            dma(2, ny, CHUNKS), dma(2, ny, half - 1, CHUNKS), dma(2, ny, CHUNKS),
            dma(2, ny, nx - 1, PIECES), dma(2, 2, ny, PIECES), dma(2, 2, nx - 1, PIECES),
        ],
        compiler_params=pltpu.CompilerParams(
            collective_id=0, has_side_effects=True, vmem_limit_bytes=60 * 2**20
        ),
    )(tokens, grad_out, w_in, w_out)
    tok_all, grad_all = tok_all.reshape(-1, width), grad_all.reshape(-1, width)
    act_all, d_pre_all = act_all.reshape(-1, hidden), d_pre_all.reshape(-1, hidden)
    win_grad, wout_grad = weight_grads(tok_all, d_pre_all, act_all, grad_all, scale)
    return mlp_out, tok_grad, win_grad, wout_grad


def solution(mesh):
    rows_spec = P(("gx", "gy"), "gz")
    in_spec = P("gz", ("gy", "gx"))
    out_spec = P(("gy", "gx"), "gz")
    sizes = (mesh.shape["gx"], mesh.shape["gy"], mesh.shape["gz"])
    return jax.shard_map(
        functools.partial(per_device, *sizes),
        mesh=mesh,
        in_specs=(rows_spec, rows_spec, in_spec, out_spec),
        out_specs=(rows_spec, rows_spec, in_spec, out_spec),
        check_vma=False,
    )
```

time: 117 us -> 88.6 us (0.76)
  Pallas kernels: 111 us -> 86.3 us
  local copies, waits for them, and re-layouts: 5.58 us -> 1.36 us
    pallas_call x1, Pallas kernels: 101 us -> 75.8 us  [per_device(): pl.pallas_call(functools.partial(ring_kernel, nx, ny, nz), out_shape=(sha...]
    unnamed x12 -> x6, local copies, waits for them, and re-layouts: 5.58 us -> 1.36 us
    pallas_call x1, Pallas kernels: 9.31 us -> 10.5 us  [weight_grads(): pl.pallas_call(functools.partial(grad_kernel, scale), grid=(steps,), out_...]
where the time goes in v2:
time: 88.6 us; the launch traced here: 88.4 us
  Pallas kernels  86.3 us (97%)
  local copies, waits for them, and re-layouts  1.36 us (2%)
    pallas_call x1, Pallas kernels, per_device(): pl.pallas_call(functools.partial(ring_kernel, nx, ny, nz), out_shape=(sha...  75.8 us
    pallas_call x1, Pallas kernels, weight_grads(): pl.pallas_call(functools.partial(grad_kernel, scale), grid=(steps,), out_...  10.5 us

profile of v2, /device:TPU:0, one launch (start us, length us, event | category | flops | bytes accessed | tf_op | source)
XLA Modules:
  0.0 88.4 jit_solution(3312237693212486810)
XLA Ops:
  0.6 75.8 %shard_map.75 = (bf16[64,1536]{1,0:T(8,128)(2,1)}, bf16[64,1536]{1,0:T(8,128)(2,1)}, bf16[4,2,64,1536]{3,2,1,0:T(8,128)(2,1)}, bf16[4,2,64,1536]{3,2,1,0:T(8,128...) custom-call(bf16[64,1536]{1,0:T(8,128)(2,1)} %tok_ref.1, bf16[64,1536]{1,0:T(8,128)(2,1)} %grad_ref.1, ...), custom_call_target="tpu_custom_call" | custom-call | tf_op jit(solution)/shard_map/pallas_call | solution.py:440
  76.5 0.0 copy-start.1
  76.5 0.0 copy-start
  76.5 10.5 %shard_map.76 = (f32[1536,1536]{1,0:T(8,128)}, f32[1536,1536]{1,0:T(8,128)}) custom-call(bf16[512,1536]{1,0:T(8,128)(2,1)} %bitcast.4, bf16[512,1536]{1,0:T(8,128)(2,1)} %bitcast.7, bf16[512,1536]{1,0:T(8,128)(2,1)} %bitcast.6, bf16[512,1536]{1,0:T(8,128)(2,1)} %bitcast.5), custom_call_target="tpu_custom_call" | custom-call | flops 4831838208 | bytes 25165824 | tf_op jit(solution)/shard_map/pallas_call | solution.py:405
  87.0 0.0 copy-done.1
  87.0 0.7 copy.10
  87.7 0.0 copy-done
  87.7 0.7 copy.11
Async XLA Ops:
  76.5 10.5 %copy-start.1 = (bf16[64,1536]{1,0:T(8,128)(2,1)S(1)}, bf16[64,1536]{1,0:T(8,128)(2,1)}, u32[]{:S(2)}) copy-start(bf16[64,1536]{1,0:T(8,128)(2,1)} %get-tuple-element.24) | copy-start | bytes 589828
  76.5 11.2 %copy-start = (bf16[64,1536]{1,0:T(8,128)(2,1)S(1)}, bf16[64,1536]{1,0:T(8,128)(2,1)}, u32[]{:S(2)}) copy-start(bf16[64,1536]{1,0:T(8,128)(2,1)} %get-tuple-element.25) | copy-start | bytes 589828

commit v3 on v2

--- a/solution.py
+++ b/solution.py
@@ -11,25 +11,35 @@
 MESH = pl.DeviceIdType.MESH
 F32, BF16 = jnp.float32, jnp.bfloat16
 
-GATHER_VIA = (False, False)
+GATHER_VIA = (False, True)
 REDUCE_VIA = (True, False)
 PIECES = 2
 CHUNKS = 2
 WIDE = 768
-FLUSHES = 2
-PLAN = (
-    "Y000", "Z000", "Y001", "Z001", "W100", "Y100", "F010", "W000", "Z100", "T100", "C000",
-    "C001", "F020", "F011", "P000", "P001", "F021", "T101", "F030", "C020", "J000", "F031",
-    "F110", "Z101", "J001", "C010", "C100", "C011", "P010", "T000", "J010", "C021", "F120",
-    "P020", "G000", "P011", "C030", "F111", "J020", "P021", "J011", "F121", "C031", "P030",
-    "G010", "P031", "J030", "F130", "C110", "J031", "G001", "J021", "G020", "F131", "C111",
-    "G011", "Y101", "P110", "C120", "C121", "P120", "P121", "G030", "E010", "G031", "J110",
-    "E011", "P111", "C130", "E030", "C131", "G021", "P130", "P131", "E031", "C101", "J130",
-    "E020", "E000", "J131", "J120", "E021", "G110", "R030", "T001", "R031", "X000", "G130",
-    "G131", "J121", "P100", "E130", "R020", "J111", "P101", "G120", "E131", "R010", "R021",
-    "J100", "G121", "E120", "G111", "E121", "E110", "R130", "J101", "E111", "R000", "G100",
-    "R131", "E001", "R120", "X001", "G101", "R110", "E100", "R121", "R011", "E101", "R111",
-    "R001", "R100", "R101",
+KINDS = "YZFCWTPJGEXR"
+PLANS = (
+    (
+        1000, 1001, 2000, 2001, 3010, 1100, 2100, 5000, 2101, 4000, 4001, 3011, 4010, 3020,
+        4100, 3021, 5100, 3030, 4011, 7010, 8010, 7000, 8000, 4020, 3031, 4021, 7020, 7011,
+        7021, 1101, 8020, 8011, 9010, 4030, 3110, 3130, 4031, 8021, 3131, 6100, 7030, 7001,
+        7031, 4101, 9020, 8030, 9011, 3120, 6101, 9000, 8031, 8001, 3111, 4130, 9021, 3121,
+        4131, 10010, 7130, 10020, 7100, 7131, 12010, 9030, 10021, 8100, 10011, 4120, 9031, 8130,
+        4121, 7120, 7101, 4110, 4111, 8131, 10030, 9001, 7110, 10031, 12020, 10000, 11000, 7111,
+        10001, 7121, 8120, 12011, 6000, 8121, 8110, 11001, 9130, 9100, 9131, 12030, 6001, 12031,
+        10130, 8111, 9120, 12021, 10131, 8101, 9121, 10120, 12130, 10121, 9110, 9111, 12131, 10110,
+        12120, 9101, 10111, 10100, 12121, 10101, 12110, 12000, 12111, 12001, 12100, 12101,
+    ),
+    (
+        1000, 1001, 2000, 2001, 3020, 3010, 3011, 3021, 4000, 5000, 3120, 3030, 3121, 4010,
+        3031, 3130, 4011, 4001, 5100, 7010, 7000, 8010, 4020, 1100, 4021, 2100, 7020, 3131,
+        2101, 8020, 4030, 1101, 7011, 8000, 7021, 9010, 3110, 8011, 4031, 6100, 7030, 7001,
+        7031, 9020, 8021, 8030, 3111, 9000, 8031, 4130, 4120, 9011, 4100, 6101, 9021, 4131,
+        8001, 4101, 10010, 7130, 10020, 7100, 4110, 7131, 10021, 10011, 9030, 9031, 4121, 8130,
+        4111, 7120, 7101, 10030, 9001, 8131, 7110, 10031, 10000, 11000, 8120, 7111, 10001, 7121,
+        8110, 6000, 12010, 8121, 9130, 11001, 9131, 6001, 9120, 10130, 8100, 10131, 8111, 12030,
+        9110, 8101, 9121, 10120, 12031, 10121, 12011, 9111, 12020, 12000, 9100, 10110, 12130, 9101,
+        10111, 10100, 12131, 12021, 10101, 12110, 12120, 12001, 12111, 12121, 12100, 12101,
+    ),
 )
 
 
@@ -55,12 +65,34 @@
     for arr in range(2):
         steps += [("R", arr, i) for i in reversed(range(ny))]
     steps = [(*step, p) for step in steps for p in range(PIECES) if step[0] != "W" or p == 0]
+    plans = (steps, steps)
     if ny == 4:
-        steps = [(step[0], *map(int, step[1:])) for step in PLAN]
+        plans = [
+            [
+                (KINDS[step // 1000 - 1], step // 100 % 10, step // 10 % 10, step % 10)
+                for step in plan
+            ]
+            for plan in PLANS
+        ]
+    cut = []
+    for plan in plans:
+        parts = [[]]
+        for step in plan:
+            if step[0] in "PET":
+                parts += [step, []]
+            else:
+                parts[-1].append(step)
+        cut.append(parts)
+    out = []
+    for ends, inside in zip(*cut):
+        if ends == inside:
+            out.append(([], [], [ends] if isinstance(ends, tuple) else ends))
+        else:
+            out.append((ends, inside, []))
     for arr in range(2):
-        last = max(at for at, step in enumerate(steps) if step[:2] == ("E", arr))
-        steps.insert(last + 1, ("S", arr, 0, 0))
-    return steps
+        last = max(at for at, part in enumerate(out) if part[2] and part[2][0][:2] == ("E", arr))
+        out.insert(last + 1, ([], [], [("S", arr, 0, 0)]))
+    return out
 
 
 def ring_kernel(
@@ -69,8 +101,9 @@
     mlp_ref, tgrad_ref, tok_out, grad_out, act_out, dpre_out,
     rows_all, win, wout, win_t, wout_t, part, pair_in, paired, part_in, slope, hid,
     mine_sum, cross, y_in, z_in, v_in, fold,
-    local, a_y, a_z, a_v, p_sem, b_sem, c_sem, d_y, d_z, d_v,
+    local, *pairs,
 ):
+    a_y, a_z, a_v, p_sem, b_sem, c_sem, d_y, d_z, d_v = zip(pairs[::2], pairs[1::2])
     x, y, z = lax.axis_index("gx"), lax.axis_index("gy"), lax.axis_index("gz")
     t, width = tok_ref.shape
     hidden = win_ref.shape[1]
@@ -80,7 +113,7 @@
     chunks = CHUNKS if hidden % (128 * CHUNKS) == 0 else 1
     core, chip = lax.rem(z, 2), lax.div(z, 2)
     partner = z + 1 - 2 * core
-    sends = []
+    sends = {}
 
     def pick(values):
         total = 0
@@ -94,6 +127,7 @@
     gaps = [{abs(table[at][i] - at) for at in range(ny)} for i in range(ny)]
     heading = [jnp.where(near[i] < y, 0, 1) for i in range(ny)]
     step_of = [1 - 2 * heading[i] for i in range(ny)]
+    back = [1 - heading[i] for i in range(ny)]
     beyond = [
         jnp.logical_or(
             jnp.logical_and(near[i] < y, y < ny - 1), jnp.logical_and(near[i] > y, y > 0)
@@ -101,13 +135,39 @@
         for i in range(ny)
     ]
     has_up, has_down = y < ny - 1, y > 0
-
-    def via(flags, arr, i):
+    at_end = jnp.logical_or(y == 0, y == ny - 1)
+    inside = jnp.logical_not(at_end)
+    role = [None]
+
+    def negate(pred):
+        return (not pred) if isinstance(pred, bool) else jnp.logical_not(pred)
+
+    def by_line_anywhere(flags, arr, i):
         if not flags[arr] or i == 0 or 1 not in gaps[i]:
             return False
-        if gaps[i] == {1}:
-            return True
-        return gap[i] == 1
+        return True if gaps[i] == {1} else gap[i] == 1
+
+    lines = {}
+    for flags in (GATHER_VIA, REDUCE_VIA):
+        for arr in range(2):
+            for i in range(ny):
+                found = by_line_anywhere(flags, arr, i)
+                lines[flags, arr, i] = (found, negate(found))
+
+    def via(flags, arr, i):
+        if role[0] is None:
+            return lines[flags, arr, i]
+        here = abs(order_table(ny)[1 if role[0] == "inside" else 0][i] - (role[0] == "inside"))
+        return (flags[arr] and here == 1), not (flags[arr] and here == 1)
+
+    def onward(i):
+        return {None: beyond[i], "end": False, "inside": True}[role[0]]
+
+    def upward():
+        return True if role[0] == "inside" else has_up
+
+    def downward():
+        return True if role[0] == "inside" else has_down
 
     def when(pred, body):
         if pred is True:
@@ -115,24 +175,30 @@
         elif pred is not False:
             pl.when(pred)(body)
 
-    def negate(pred):
-        return (not pred) if isinstance(pred, bool) else jnp.logical_not(pred)
-
-    def remote(src, dst, sems, index, device):
+    def remote(src, dst, leaving, landing, device):
         return pltpu.make_async_remote_copy(
-            src_ref=src, dst_ref=dst, send_sem=sems.at[(0, *index)],
-            recv_sem=sems.at[(1, *index)], device_id=device, device_id_type=MESH,
+            src_ref=src, dst_ref=dst, send_sem=leaving, recv_sem=landing,
+            device_id=device, device_id_type=MESH,
         )
 
-    def send(src, dst, sems, index, device, pred=True):
-        if pred is False:
+    def send(src, dst, sems, index, device, pred=lambda: True, leaving=None, bulk=None, key=None):
+        now = pred()
+        if now is False:
             return
-        copy = remote(src, dst, sems, index, device)
-        when(pred, copy.start)
-        sends.append((pred, copy))
+        leaving = index[:-1] if leaving is None else leaving
+        copy = remote(src, dst, sems[0].at[leaving], sems[1].at[index], device)
+        when(now, copy.start)
+        sends.setdefault(key, (sems, leaving, index, bulk, pred))
 
     def arrive(ref, sems, index):
-        remote(ref, ref, sems, index, {"gz": z}).wait_recv()
+        leaving = sems[0].at[(0,) * len(sems[0].shape)]
+        remote(ref, ref, leaving, sems[1].at[index], {"gz": z}).wait_recv()
+
+    def depart():
+        for sems, leaving, index, bulk, pred in sends.values():
+            ref = rows_all.at[0, 0, 0] if bulk is None else bulk
+            copy = remote(ref, ref, sems[0].at[leaving], sems[1].at[index], {"gz": z})
+            when(pred(), copy.wait_send)
 
     def peer(e):
         return {"gx": lax.rem(x + e, nx)}
@@ -169,11 +235,13 @@
     pl.semaphore_wait(barrier, nx + ny + nz - 3)
     stores = []
 
-    def to_columns(arr, i, p, pred=True):
+    def to_columns(arr, i, p, pred=lambda: True):
         block = rows_all.at[arr, near[i], 0, :, piece(p)]
         for e in range(1, nx):
             dst = rows_all.at[arr, near[i], nx - e, :, piece(p)]
-            send(block, dst, a_y, (arr, i, nx - e - 1, p), peer(e), pred)
+            send(
+                block, dst, a_y, (arr, i, nx - e - 1, p), peer(e), pred, key=("a_y", arr, i, e)
+            )
 
     def own_columns(arr, i, p):
         if p == 0:
@@ -182,27 +250,33 @@
 
     def own_line(arr, i, p):
         block = rows_all.at[arr, y, 0, :, piece(p)]
-        send(block, block, a_z, (arr, 0, y, p), {"gy": y + 1}, has_up)
-        send(block, block, a_z, (arr, 1, y, p), {"gy": y - 1}, has_down)
+        for turn, to, pred in ((0, y + 1, upward), (1, y - 1, downward)):
+            send(
+                block, block, a_z, (arr, y, p), {"gy": to}, pred, (arr, turn, y),
+                key=("a_z", arr, turn),
+            )
 
     def own_column(arr, i, p):
         block = rows_all.at[arr, near[i], 0, :, piece(p)]
-        arrive(block, a_z, (arr, heading[i], near[i], p))
+        arrive(block, a_z, (arr, near[i], p))
         send(
-            block, block, a_z, (arr, heading[i], near[i], p),
-            {"gy": y + step_of[i]}, beyond[i],
+            block, block, a_z, (arr, near[i], p), {"gy": y + step_of[i]}, lambda: onward(i),
+            (arr, heading[i], near[i]), key=("a_z", arr, i, 0),
         )
-        to_columns(arr, i, p, negate(via(GATHER_VIA, arr, i)))
+        to_columns(arr, i, p, lambda: via(GATHER_VIA, arr, i)[1])
 
     def other_columns(arr, i, p):
-        by_line = via(GATHER_VIA, arr, i)
+        by_line, by_column = via(GATHER_VIA, arr, i)
         for e in range(1, nx):
             block = rows_all.at[arr, near[i], e, :, piece(p)]
             when(by_line, lambda: arrive(block, a_v, (arr, heading[i], e - 1, p)))
-            when(negate(by_line), lambda: arrive(block, a_y, (arr, i, e - 1, p)))
+            when(by_column, lambda: arrive(block, a_y, (arr, i, e - 1, p)))
             if i == 0 and GATHER_VIA[arr]:
-                send(block, block, a_v, (arr, 0, e - 1, p), {"gy": y + 1}, has_up)
-                send(block, block, a_v, (arr, 1, e - 1, p), {"gy": y - 1}, has_down)
+                for turn, to, pred in ((0, y + 1, upward), (1, y - 1, downward)):
+                    send(
+                        block, block, a_v, (arr, turn, e - 1, p), {"gy": to}, pred,
+                        key=("a_v", arr, turn, e),
+                    )
 
     def turn_over(arr, i, p):
         src, dst = ((win, win_t), (wout, wout_t))[arr]
@@ -225,7 +299,7 @@
         tiles(hidden // chunks, body, c * (hidden // chunks), WIDE)
         send(
             part.at[arr, i, 1 - core, :, chunk(c)], pair_in.at[arr, i, :, chunk(c)],
-            p_sem, (arr, i, c), {"gz": partner},
+            p_sem, (arr, i, c), {"gz": partner}, leaving=(0,), bulk=pair_in, key="p",
         )
 
     def join(arr, i, c):
@@ -240,7 +314,8 @@
             to = lax.rem(chip + d, half)
             send(
                 paired.at[arr, i, :, chunk(c)], part_in.at[arr, i, d - 1, :, chunk(c)],
-                b_sem, (arr, i, d - 1, c), {"gz": 2 * to + core},
+                b_sem, (arr, i, d - 1, c), {"gz": 2 * to + core}, leaving=(0,), bulk=part_in,
+                key="b",
             )
 
     def activate(arr, i, c):
@@ -260,7 +335,9 @@
             arrive(part_in.at[arr, i, d - 1, :, chunk(c)], b_sem, (arr, i, d - 1, c))
         tiles(hidden // chunks, body, c * (hidden // chunks))
         mine = hid.at[arr, i, core, :, chunk(c)]
-        send(mine, mine, c_sem, (arr, i, c), {"gz": partner})
+        send(
+            mine, mine, c_sem, (arr, i, c), {"gz": partner}, leaving=(0,), bulk=pair_in, key="c"
+        )
 
     def expand(arr, i, p):
         if p == 0:
@@ -275,27 +352,26 @@
             for e in range(1, nx):
                 cross[arr, i, e - 1, :, cols] = out[e * t:(e + 1) * t].astype(BF16)
 
-        by_line = via(REDUCE_VIA, arr, i)
         tiles(width // PIECES, body, p * (width // PIECES), WIDE)
         if i == 0 and REDUCE_VIA[arr]:
             return
         for e in range(1, nx):
             src = cross.at[arr, i, e - 1, :, piece(p)]
-            turn = 1 - heading[i]
             send(
-                src, v_in.at[arr, turn, e - 1, :, piece(p)], d_v, (arr, turn, e - 1, p),
-                {"gy": y - step_of[i]}, by_line,
+                src, v_in.at[arr, back[i], e - 1, :, piece(p)], d_v, (arr, back[i], e - 1, p),
+                {"gy": y - step_of[i]}, lambda: via(REDUCE_VIA, arr, i)[0],
+                key=("d_v", arr, i, e),
             )
             send(
                 src, y_in.at[arr, i, nx - e - 1, :, piece(p)], d_y, (arr, i, nx - e - 1, p),
-                peer(e), negate(by_line),
+                peer(e), lambda: via(REDUCE_VIA, arr, i)[1], key=("d_y", arr, i, e),
             )
 
     def own_cross(arr, i, p):
         if not REDUCE_VIA[arr]:
             return
         for e in range(1, nx):
-            for turn, pred in ((0, has_down), (1, has_up)):
+            for turn, pred in ((0, downward()), (1, upward())):
                 def take(turn=turn):
                     got = v_in.at[arr, turn, e - 1, :, piece(p)]
                     arrive(got, d_v, (arr, turn, e - 1, p))
@@ -311,12 +387,10 @@
             src = cross.at[arr, 0, e - 1, :, piece(p)]
             send(
                 src, y_in.at[arr, 0, nx - e - 1, :, piece(p)], d_y, (arr, 0, nx - e - 1, p),
-                peer(e),
+                peer(e), key=("d_y", arr, 0, e),
             )
 
     def reduce(arr, i, p):
-        by_line = via(REDUCE_VIA, arr, i)
-
         def from_columns():
             for e in range(1, nx):
                 arrive(y_in.at[arr, i, e - 1, :, piece(p)], d_y, (arr, i, e - 1, p))
@@ -339,22 +413,21 @@
             tiles(width // PIECES, body, p * (width // PIECES))
 
         out = (mlp_ref, tgrad_ref)[arr]
-        when(negate(by_line), from_columns)
+        when(via(REDUCE_VIA, arr, i)[1], from_columns)
         if i == 0:
-            when(has_down, lambda: from_line(0, y))
-            when(has_up, lambda: from_line(1, y))
+            when(downward(), lambda: from_line(0, y))
+            when(upward(), lambda: from_line(1, y))
             out[:, piece(p)] = mine_sum[arr, 0, :, piece(p)].astype(BF16)
             return
-        turn = 1 - heading[i]
-        when(beyond[i], lambda: from_line(turn, near[i]))
+        when(onward(i), lambda: from_line(back[i], near[i]))
 
         def body(cols):
             fold[arr, i, :, cols] = mine_sum[arr, i, :, cols].astype(BF16)
 
         tiles(width // PIECES, body, p * (width // PIECES))
         send(
-            fold.at[arr, i, :, piece(p)], z_in.at[arr, turn, near[i], :, piece(p)],
-            d_z, (arr, turn, near[i], p), {"gy": y - step_of[i]},
+            fold.at[arr, i, :, piece(p)], z_in.at[arr, back[i], near[i], :, piece(p)],
+            d_z, (arr, back[i], near[i], p), {"gy": y - step_of[i]}, key=("d_z", arr, i),
         )
 
     def store(arr, i, p):
@@ -372,58 +445,96 @@
         "P": project, "J": join, "G": activate, "E": expand, "X": own_cross, "R": reduce,
         "S": store, "W": lambda arr, i, p: stage[2 + arr].wait(),
     }
-    def flush(count):
-        for pred, copy in sends[:count]:
-            when(pred, copy.wait_send)
-        del sends[:count]
-
-    steps = schedule(ny)
-    marks = [at for at, step in enumerate(steps) if step[0] == "R"][-FLUSHES:]
-    before = 0
-    for at, (name, arr, i, p) in enumerate(steps):
-        if name in "PJG" and p >= chunks:
-            continue
-        if at in marks:
-            flush(before)
-        before = len(sends)
-        acts[name](arr, i, p)
-    flush(len(sends))
+    def run(steps):
+        for name, arr, i, p in steps:
+            if name not in "PJG" or p < chunks:
+                acts[name](arr, i, p)
+
+    def run_at(steps, place, pred):
+        def body():
+            role[0] = place
+            run(steps)
+            role[0] = None
+
+        if steps:
+            pl.when(pred)(body)
+
+    for at_ends, insides, both in schedule(ny):
+        run_at(at_ends, "end", at_end)
+        run_at(insides, "inside", inside)
+        run(both)
+    depart()
     for copy in stores:
         copy.wait()
 
 
-def grad_kernel(scale, tok_ref, dpre_ref, act_ref, grad_ref, win_ref, wout_ref):
-    win_ref[...] = contract(tok_ref[...], dpre_ref[...], ((0,), (0,))) * scale
-    wout_ref[...] = contract(act_ref[...], grad_ref[...], ((0,), (0,))) * scale
-
-
-def weight_grads(tok, dpre, act, grad, scale):
+def grad_kernel(
+    scale, tok_ref, dpre_ref, act_ref, grad_ref, mlp_ref, tgrad_ref,
+    win_ref, wout_ref, mlp_out, tgrad_out,
+    tok, dpre, act, grad, rows, win, wout, loads, stores,
+):
+    def load(src, dst, at):
+        copy = pltpu.make_async_copy(src, dst, loads.at[at])
+        copy.start()
+        return copy
+
+    first = [load(tok_ref, tok, 0), load(dpre_ref, dpre, 1)]
+    second = [load(act_ref, act, 2), load(grad_ref, grad, 3)]
+    passing = [load(mlp_ref, rows.at[0], 4), load(tgrad_ref, rows.at[1], 5)]
+
+    def product(left, right, total, out, sem):
+        tall = next(n for n in (256, 128) if total.shape[0] % n == 0)
+
+        def step(i, carry):
+            part = pl.ds(pl.multiple_of(i * tall, 128), tall)
+            total[part, :] = contract(left[:, part], right[...], ((0,), (0,))) * scale
+            pltpu.make_async_copy(total.at[part, :], out.at[part, :], sem).start()
+            return carry
+
+        count = total.shape[0] // tall
+        lax.fori_loop(0, count, step, 0, unroll=2 if count % 2 == 0 else 1)
+
+    for copy in first:
+        copy.wait()
+    product(tok, dpre, win, win_ref, stores.at[0])
+    for copy in second:
+        copy.wait()
+    product(act, grad, wout, wout_ref, stores.at[1])
+    for at, out in enumerate((mlp_out, tgrad_out)):
+        passing[at].wait()
+        pltpu.make_async_copy(rows.at[at], out, stores.at[2 + at]).start()
+    pltpu.make_async_copy(win, win_ref, stores.at[0]).wait()
+    pltpu.make_async_copy(wout, wout_ref, stores.at[1]).wait()
+    for at, out in enumerate((mlp_out, tgrad_out)):
+        pltpu.make_async_copy(rows.at[at], out, stores.at[2 + at]).wait()
+
+
+def finish(tok, dpre, act, grad, mlp, tgrad, scale):
     tokens, width = tok.shape
     hidden = dpre.shape[1]
-    steps = next(n for n in (6, 3, 2, 1) if width % (128 * n) == 0 and hidden % (128 * n) == 0)
-    wide, tall = width // steps, hidden // steps
+    shape = jax.ShapeDtypeStruct
+    anywhere = pl.BlockSpec(memory_space=pl.ANY)
     return pl.pallas_call(
         functools.partial(grad_kernel, scale),
-        grid=(steps,),
         out_shape=(
-            jax.ShapeDtypeStruct((width, hidden), F32), jax.ShapeDtypeStruct((hidden, width), F32),
+            shape((width, hidden), F32), shape((hidden, width), F32),
+            shape(mlp.shape, BF16), shape(tgrad.shape, BF16),
         ),
-        in_specs=[
-            pl.BlockSpec((tokens, wide), lambda i: (0, i)),
-            pl.BlockSpec((tokens, hidden), lambda i: (0, 0)),
-            pl.BlockSpec((tokens, tall), lambda i: (0, i)),
-            pl.BlockSpec((tokens, width), lambda i: (0, 0)),
+        in_specs=[anywhere] * 6,
+        out_specs=(anywhere,) * 4,
+        scratch_shapes=[
+            pltpu.VMEM(tok.shape, BF16), pltpu.VMEM(dpre.shape, BF16),
+            pltpu.VMEM(act.shape, BF16), pltpu.VMEM(grad.shape, BF16),
+            pltpu.VMEM((2, *mlp.shape), BF16),
+            pltpu.VMEM((width, hidden), F32), pltpu.VMEM((hidden, width), F32),
+            pltpu.SemaphoreType.DMA((6,)), pltpu.SemaphoreType.DMA((4,)),
         ],
-        out_specs=(
-            pl.BlockSpec((wide, hidden), lambda i: (i, 0)),
-            pl.BlockSpec((tall, width), lambda i: (i, 0)),
-        ),
         compiler_params=pltpu.CompilerParams(vmem_limit_bytes=60 * 2**20),
         cost_estimate=pl.CostEstimate(
             flops=4 * tokens * width * hidden, transcendentals=0,
             bytes_accessed=8 * width * hidden + 4 * tokens * (width + hidden),
         ),
-    )(tok, dpre, act, grad)
+    )(tok, dpre, act, grad, mlp, tgrad)
 
 
 def per_device(nx, ny, nz, tokens, grad_out, w_in, w_out):
@@ -435,7 +546,7 @@
     scale = 1.0 / math.sqrt(ny * t)
     anywhere = pl.BlockSpec(memory_space=pl.ANY)
     vmem = pl.BlockSpec(memory_space=pltpu.VMEM)
-    dma = lambda *shape: pltpu.SemaphoreType.DMA((2, *shape))
+    dma = lambda *shape: pltpu.SemaphoreType.DMA(shape)
     shape = jax.ShapeDtypeStruct
     mlp_out, tok_grad, tok_all, grad_all, act_all, d_pre_all = pl.pallas_call(
         functools.partial(ring_kernel, nx, ny, nz),
@@ -465,9 +576,11 @@
             pltpu.VMEM((2, 2, nx - 1, t, width), BF16),
             pltpu.VMEM((2, ny, t, width), BF16),
             pltpu.SemaphoreType.DMA((6 + 2 * ny,)),
-            dma(2, ny, nx - 1, PIECES), dma(2, 2, ny, PIECES), dma(2, 2, nx - 1, PIECES),
-            dma(2, ny, CHUNKS), dma(2, ny, half - 1, CHUNKS), dma(2, ny, CHUNKS),
-            dma(2, ny, nx - 1, PIECES), dma(2, 2, ny, PIECES), dma(2, 2, nx - 1, PIECES),
+            dma(2, ny, nx - 1), dma(2, ny, nx - 1, PIECES), dma(2, 2, ny), dma(2, ny, PIECES),
+            dma(2, 2, nx - 1), dma(2, 2, nx - 1, PIECES), dma(1), dma(2, ny, CHUNKS),
+            dma(1), dma(2, ny, half - 1, CHUNKS), dma(1), dma(2, ny, CHUNKS),
+            dma(2, ny, nx - 1), dma(2, ny, nx - 1, PIECES), dma(2, 2, ny), dma(2, 2, ny, PIECES),
+            dma(2, 2, nx - 1), dma(2, 2, nx - 1, PIECES),
         ],
         compiler_params=pltpu.CompilerParams(
             collective_id=0, has_side_effects=True, vmem_limit_bytes=60 * 2**20
@@ -475,7 +588,9 @@
     )(tokens, grad_out, w_in, w_out)
     tok_all, grad_all = tok_all.reshape(-1, width), grad_all.reshape(-1, width)
     act_all, d_pre_all = act_all.reshape(-1, hidden), d_pre_all.reshape(-1, hidden)
-    win_grad, wout_grad = weight_grads(tok_all, d_pre_all, act_all, grad_all, scale)
+    win_grad, wout_grad, mlp_out, tok_grad = finish(
+        tok_all, d_pre_all, act_all, grad_all, mlp_out, tok_grad, scale
+    )
     return mlp_out, tok_grad, win_grad, wout_grad
 
 

time: 88.6 us -> 81.3 us (0.918)
  Pallas kernels: 86.3 us -> 80.4 us
  local copies, waits for them, and re-layouts: 1.36 us -> 0 us
    pallas_call x1, Pallas kernels: 75.8 us -> 71 us  [per_device(): pl.pallas_call(functools.partial(ring_kernel, nx, ny, nz), out_shape=(sha...]
    unnamed x6 -> x0, local copies, waits for them, and re-layouts: 1.36 us -> none
    pallas_call x1, Pallas kernels: 10.5 us -> 9.32 us  [finish(): pl.pallas_call(functools.partial(grad_kernel, scale), out_shape=(shape((w...]
where the time goes in v3:
time: 81.3 us; the launch traced here: 81.2 us
  Pallas kernels  80.4 us (99%)
    pallas_call x1, Pallas kernels, per_device(): pl.pallas_call(functools.partial(ring_kernel, nx, ny, nz), out_shape=(sha...  71 us
    pallas_call x1, Pallas kernels, finish(): pl.pallas_call(functools.partial(grad_kernel, scale), out_shape=(shape((w...  9.32 us

profile of v3, /device:TPU:0, one launch (start us, length us, event | category | flops | bytes accessed | tf_op | source)
XLA Modules:
  0.0 81.2 jit_solution(10329868201734890622)
XLA Ops:
  0.6 71.0 %shard_map.75 = (bf16[64,1536]{1,0:T(8,128)(2,1)}, bf16[64,1536]{1,0:T(8,128)(2,1)}, bf16[4,2,64,1536]{3,2,1,0:T(8,128)(2,1)}, bf16[4,2,64,1536]{3,2,1,0:T(8,128...) custom-call(bf16[64,1536]{1,0:T(8,128)(2,1)} %tok_ref.1, bf16[64,1536]{1,0:T(8,128)(2,1)} %grad_ref.1, ...), custom_call_target="tpu_custom_call" | custom-call | tf_op jit(solution)/shard_map/pallas_call | solution.py:551
  71.7 9.3 %shard_map.76 = (f32[1536,1536]{1,0:T(8,128)}, f32[1536,1536]{1,0:T(8,128)}, bf16[64,1536]{1,0:T(8,128)(2,1)}, bf16[64,1536]{1,0:T(8,128)(2,1)}) custom-call(bf16[512,1536]{1,0:T(8,128)(2,1)} %bitcast.4, bf16[512,1536]{1,0:T(8,128)(2,1)} %bitcast.7, bf16[512,1536]{1,0:T(8,128)(2,1)} %bitcast.6, bf16[512,1536]{1,0:T(8,128)(2,1)} %bitcast.5, ...), custom_call_target="tpu_custom_call" | custom-call | flops 4831838208 | bytes 25165824 | tf_op jit(solution)/shard_map/pallas_call | solution.py:517

commit v4 on v3

--- a/solution.py
+++ b/solution.py
@@ -479,8 +479,6 @@
         return copy
 
     first = [load(tok_ref, tok, 0), load(dpre_ref, dpre, 1)]
-    second = [load(act_ref, act, 2), load(grad_ref, grad, 3)]
-    passing = [load(mlp_ref, rows.at[0], 4), load(tgrad_ref, rows.at[1], 5)]
 
     def product(left, right, total, out, sem):
         tall = next(n for n in (256, 128) if total.shape[0] % n == 0)
@@ -496,6 +494,8 @@
 
     for copy in first:
         copy.wait()
+    second = [load(act_ref, act, 2), load(grad_ref, grad, 3)]
+    passing = [load(mlp_ref, rows.at[0], 4), load(tgrad_ref, rows.at[1], 5)]
     product(tok, dpre, win, win_ref, stores.at[0])
     for copy in second:
         copy.wait()

time: 81.3 us -> 81.3 us (level)
  no operation moved by 1% of the time
where the time goes in v4:
time: 81.3 us; the launch traced here: 81.2 us
  Pallas kernels  80.4 us (99%)
    pallas_call x1, Pallas kernels, per_device(): pl.pallas_call(functools.partial(ring_kernel, nx, ny, nz), out_shape=(sha...  71 us
    pallas_call x1, Pallas kernels, finish(): pl.pallas_call(functools.partial(grad_kernel, scale), out_shape=(shape((w...  9.32 us

profile of v4, /device:TPU:0, one launch (start us, length us, event | category | flops | bytes accessed | tf_op | source)
XLA Modules:
  0.0 81.2 jit_solution(18347754719647453845)
XLA Ops:
  0.6 71.0 %shard_map.75 = (bf16[64,1536]{1,0:T(8,128)(2,1)}, bf16[64,1536]{1,0:T(8,128)(2,1)}, bf16[4,2,64,1536]{3,2,1,0:T(8,128)(2,1)}, bf16[4,2,64,1536]{3,2,1,0:T(8,128...) custom-call(bf16[64,1536]{1,0:T(8,128)(2,1)} %tok_ref.1, bf16[64,1536]{1,0:T(8,128)(2,1)} %grad_ref.1, ...), custom_call_target="tpu_custom_call" | custom-call | tf_op jit(solution)/shard_map/pallas_call | solution.py:551
  71.7 9.3 %shard_map.76 = (f32[1536,1536]{1,0:T(8,128)}, f32[1536,1536]{1,0:T(8,128)}, bf16[64,1536]{1,0:T(8,128)(2,1)}, bf16[64,1536]{1,0:T(8,128)(2,1)}) custom-call(bf16[512,1536]{1,0:T(8,128)(2,1)} %bitcast.4, bf16[512,1536]{1,0:T(8,128)(2,1)} %bitcast.7, bf16[512,1536]{1,0:T(8,128)(2,1)} %bitcast.6, bf16[512,1536]{1,0:T(8,128)(2,1)} %bitcast.5, ...), custom_call_target="tpu_custom_call" | custom-call | flops 4831838208 | bytes 25165824 | tf_op jit(solution)/shard_map/pallas_call | solution.py:517
